TPU v7x, 32 devices: a whole 2x2x4 slice. The times are simulated.
32 devices in a mesh: elem: 8 (over z, y), chan: 4 (over x, core).
Axes of the slice: x: 2, y: 2, z: 4, core: 2. Of those that a mesh axis runs over, the one named last changes fastest.
Arguments:
- voltages: bfloat16 [2, 1024, 19584], P(None, ('elem', 'chan')), may hold values from -6 to 6
- delays: int32 [1024], P(('elem', 'chan')), may hold values from 0 to 127
- prototype: bfloat16 [16, 1024], replicated, may hold values from -1.5 to 1.5
- subband_map: int32 [16], replicated, may hold values from 0 to 1023, as said below
- beam_weights: bfloat16 [512, 2, 16, 1024], P('elem', None, 'chan'), may hold values from -0.25 to 0.25
Outputs:
- element_power: bfloat16 [1024, 1024], P(('elem', 'chan'))
- beam_voltages: float32 [2, 64, 512], P(None, 'chan', 'elem')
Inputs may be any that keep to these rules, and one draw needn't show every extreme that they name: `subband_map`: distinct channel numbers.
All inputs are finite; a program needn't handle non-finite values.
Results may differ from a plain program's by a relative error of at most 0.007.
Values may be sent and summed in bfloat16 or wider, within the bound.
A program may use at most 128 MiB of HBM per device.

v0:
```python
import functools
import math

import jax
import jax.numpy as jnp
import numpy as np
from jax import lax
from jax.experimental import pallas as pl
from jax.experimental.pallas import tpu as pltpu
from jax.sharding import PartitionSpec as P

FRAMES = 4
LANES = 128
RADIX = 8
LOGICAL = pl.DeviceIdType.LOGICAL


def cosine(turns, chan):
    y = jnp.abs((turns & (chan - 1)) - chan // 2) - chan // 4
    x = y.astype(jnp.float32) * (2.0 * math.pi / chan)
    s = x * x
    poly = 1.0 / 362880 - s * (1.0 / 39916800)
    poly = -1.0 / 5040 + s * poly
    poly = 1.0 / 120 + s * poly
    poly = -1.0 / 6 + s * poly
    return (x + x * s * poly) * (chan**-0.5)


def split(value):
    high = value.astype(jnp.bfloat16)
    return high, (value - high.astype(jnp.float32)).astype(jnp.bfloat16)


NT = (((1,), (1,)), ((), ()))


def eight_points(x):
    def add(a, b):
        return (a[0] + b[0], a[1] + b[1])

    def sub(a, b):
        return (a[0] - b[0], a[1] - b[1])

    def minus_i(a):
        return (a[1], -a[0])

    def four(v):
        a, b = add(v[0], v[2]), sub(v[0], v[2])
        c, d = add(v[1], v[3]), minus_i(sub(v[1], v[3]))
        return [add(a, c), add(b, d), sub(a, c), sub(b, d)]

    root = math.sqrt(0.5)
    even = four([add(x[a], x[a + 4]) for a in range(4)])
    d = [sub(x[a], x[a + 4]) for a in range(4)]
    d1 = ((d[1][0] + d[1][1]) * root, (d[1][1] - d[1][0]) * root)
    d3 = ((d[3][1] - d[3][0]) * root, (-d[3][0] - d[3][1]) * root)
    odd = four([d[0], d1, minus_i(d[2]), d3])
    out = []
    for e, o in zip(even, odd):
        out += [e, o]
    return out


def turn_plan(chunk, groups, rows, delay_ref):
    lane = lax.broadcasted_iota(jnp.int32, (rows, LANES), 1)
    sub = lax.broadcasted_iota(jnp.int32, (rows, LANES), 0)
    shift = jnp.zeros((rows, LANES), jnp.int32)
    for i in range(rows):
        shift = jnp.where(sub == i, delay_ref[chunk % groups * rows + i], shift)
    return (lane + shift) & (LANES - 1), lane < LANES - shift


def turn_columns(chunk, first, last, held, plan, volt_ref, seg_ref):
    index, keep = plan

    def turned(c):
        value = volt_ref[chunk, :, pl.ds(c * LANES, LANES)].astype(jnp.float32)
        return jnp.take_along_axis(value, index, axis=1, mode="promise_in_bounds")

    now = turned(first) if held is None else held
    for c in range(first, last):
        nxt = turned(c + 1)
        seg_ref[chunk % 2, :, pl.ds(c * LANES, LANES)] = jnp.where(keep, now, nxt)
        now = nxt
    return now


def filter_column(chunk, groups, j, coef_ref, seg_ref, wave_ref):
    rows = seg_ref.shape[1]
    taps, _, chan = coef_ref.shape
    per = chan // LANES
    part, group = chunk // groups, chunk % groups
    held = [
        seg_ref[chunk % 2, :, pl.ds((b * per + j) * LANES, LANES)]
        for b in range(FRAMES + taps - 1)
    ]
    sums = [None] * FRAMES
    for t in range(taps):
        coef = coef_ref[t, :, pl.ds(j * LANES, LANES)]
        for f in range(FRAMES):
            term = coef * held[f + t]
            sums[f] = term if t == 0 else sums[f] + term
    for f in range(FRAMES):
        wave_ref[part, f, pl.ds(group * rows, rows), pl.ds(j * LANES, LANES)] = sums[f].astype(
            jnp.bfloat16
        )


def main_kernel(
    nelem,
    nchan,
    delay_hbm,
    map_hbm,
    volt_hbm,
    proto_hbm,
    weight_hbm,
    basis_hbm,
    power_ref,
    beam_ref,
    delay_ref,
    map_ref,
    volt_ref,
    proto_ref,
    raw_ref,
    basis_ref,
    seg_ref,
    coef_ref,
    wave_ref,
    weight_ref,
    send_ref,
    recv_ref,
    picked_ref,
    local_sem,
    volt_sem,
    send_sem,
    recv_sem,
):
    parts, frames, elems, chan = wave_ref.shape
    chunks, chunk_rows, _ = volt_ref.shape
    groups = chunks // parts
    taps = proto_ref.shape[0]
    count = nelem * nchan
    elem_at, chan_at = lax.axis_index("elem"), lax.axis_index("chan")
    me = elem_at * nchan + chan_at
    barrier = pltpu.get_barrier_semaphore()

    def each_partner(act):
        near_start = elem_at < nelem // 2

        def row(k, carry):
            first = jnp.where(near_start, nelem - 1 - k, k) * nchan
            for c in range(nchan):

                @pl.when(first + c != me)
                def _():
                    act(first + c, c)

            return carry

        if count <= 64:
            for k in range(nelem):
                row(k, 0)
        else:
            lax.fori_loop(0, nelem, row, 0)

    map_copy = pltpu.make_async_copy(map_hbm, map_ref, local_sem.at[0])
    proto_copy = pltpu.make_async_copy(proto_hbm, proto_ref, local_sem.at[1])
    delay_copy = pltpu.make_async_copy(delay_hbm, delay_ref, local_sem.at[2])
    basis_copy = pltpu.make_async_copy(basis_hbm, basis_ref, local_sem.at[3])
    weight_copy = pltpu.make_async_copy(weight_hbm, raw_ref, local_sem.at[4])
    volt_copies = [
        pltpu.make_async_copy(
            volt_hbm.at[k // groups, pl.ds(k % groups * chunk_rows, chunk_rows)],
            volt_ref.at[k],
            volt_sem.at[k],
        )
        for k in range(chunks)
    ]
    map_copy.start()
    proto_copy.start()
    delay_copy.start()
    ahead = min(4, chunks)
    for copy in volt_copies[:ahead]:
        copy.start()

    def greet(other, c):
        pl.semaphore_signal(barrier, inc=1, device_id=other, device_id_type=LOGICAL)

    each_partner(greet)
    map_copy.wait()

    subbands = map_ref.shape[0]
    block = subbands // nchan
    rows = 2 * subbands
    row = lax.broadcasted_iota(jnp.int32, (rows, LANES), 0)
    band = (row // (2 * block)) * block + row % block
    wanted = jnp.zeros((rows, LANES), jnp.int32)
    for s in range(subbands):
        wanted = jnp.where(band == s, map_ref[s], wanted)
    quarter = ((row // block) % 2) * (chan // 4)
    lane = lax.broadcasted_iota(jnp.int32, (rows, LANES), 1)
    real_basis, imag_basis = [], []
    for j in range(chan // LANES):
        turns = wanted * (lane + j * LANES) + quarter
        real_basis.append(cosine(turns, chan))
        imag_basis.append(cosine(turns + 3 * (chan // 4), chan))
    real_basis = jnp.concatenate(split(jnp.concatenate(real_basis, axis=1)), axis=0)
    imag_basis = jnp.concatenate(split(jnp.concatenate(imag_basis, axis=1)), axis=0)
    proto_copy.wait()
    for t in range(taps):
        coef_ref[t] = jnp.broadcast_to(
            proto_ref[pl.ds(t, 1), :].astype(jnp.float32), (8, chan)
        )
    delay_copy.wait()

    per = chan // LANES
    step = (frames + taps - 1) * per // per

    def arrive(k):
        volt_copies[k].wait()
        if k + ahead < chunks:
            volt_copies[k + ahead].start()
        elif k + ahead == chunks:
            basis_copy.start()
            weight_copy.start()

    def pick(r, basis):
        return lax.dot_general(
            basis,
            wave_ref[r].reshape(frames * elems, chan),
            NT,
            preferred_element_type=jnp.float32,
        )

    arrive(0)
    plan = turn_plan(0, groups, chunk_rows, delay_ref)
    turn_columns(0, 0, step * per, None, plan, volt_ref, seg_ref)
    for k in range(chunks):
        held = None
        if k + 1 < chunks:
            arrive(k + 1)
            plan = turn_plan(k + 1, groups, chunk_rows, delay_ref)
        if k == groups:
            both = pick(0, real_basis)
        for j in range(per):
            filter_column(k, groups, j, coef_ref, seg_ref, wave_ref)
            if k + 1 < chunks:
                held = turn_columns(
                    k + 1, j * step, (j + 1) * step, held, plan, volt_ref, seg_ref
                )

    wave = [wave_ref[r].reshape(frames * elems, chan) for r in range(2)]
    both = both + pick(1, imag_basis)
    chosen = (both[:rows] + both[rows:]).astype(jnp.bfloat16)
    for c in range(nchan):
        send_ref[c] = chosen[2 * block * c : 2 * block * (c + 1)]

    pl.semaphore_wait(barrier, count - 1)

    def send(other, c):
        pltpu.make_async_remote_copy(
            src_ref=send_ref.at[c],
            dst_ref=recv_ref.at[me],
            send_sem=send_sem,
            recv_sem=recv_sem,
            device_id=other,
            device_id_type=LOGICAL,
        ).start()

    each_partner(send)
    recv_ref[me] = send_ref[chan_at]

    lanes = chan // RADIX
    split_wave = [
        tuple(wave[r][:, a * lanes : (a + 1) * lanes].astype(jnp.float32) for r in range(2))
        for a in range(RADIX)
    ]
    classes = eight_points(split_wave)
    basis_copy.wait()
    powers = []
    for c in range(RADIX):
        mixed = jnp.concatenate(classes[c], axis=1).astype(jnp.bfloat16)
        spec = jnp.dot(mixed, basis_ref[c], preferred_element_type=jnp.float32)
        both = spec[:, :lanes] * spec[:, :lanes] + spec[:, lanes:] * spec[:, lanes:]
        total = both[:elems]
        for f in range(1, frames):
            total = total + both[f * elems : (f + 1) * elems]
        powers.append(total * (1.0 / frames))
    wide = lanes // RADIX
    at = lax.broadcasted_iota(jnp.int32, (elems, lanes), 1)
    mixed = []
    for e in range(RADIX):
        piece = None
        for c in range(RADIX):
            shift = (wide * (c - e)) % lanes
            moved = pltpu.roll(powers[c], shift, 1) if shift else powers[c]
            piece = moved if piece is None else jnp.where(at // wide == c, moved, piece)
        mixed.append(piece)
    mixed = jnp.concatenate(mixed, axis=0).astype(jnp.bfloat16)
    down = lax.broadcasted_iota(jnp.int32, (lanes, lanes), 0)
    over = lax.broadcasted_iota(jnp.int32, (lanes, lanes), 1)
    order = (over == (down % wide) * RADIX + down // wide).astype(jnp.float32)
    final = jnp.dot(mixed, order.astype(jnp.bfloat16), preferred_element_type=jnp.float32)
    for e in range(RADIX):
        power_ref[:, e * lanes : (e + 1) * lanes] = final[e * elems : (e + 1) * elems].astype(
            jnp.bfloat16
        )

    weight_rows = weight_ref.shape[0]
    beams = weight_rows // (2 * block)
    down = lax.broadcasted_iota(jnp.int32, (weight_rows, 2 * beams), 0)
    over = lax.broadcasted_iota(jnp.int32, (weight_rows, 2 * beams), 1)
    gather = (down // (2 * block) == over % beams) & ((down // block) % 2 == over // beams)
    gather = gather.astype(jnp.float32).astype(jnp.bfloat16)
    weight_copy.wait()
    step = min(8, raw_ref.shape[0])
    for i in range(0, raw_ref.shape[0], step):
        piece = raw_ref[i : i + step].reshape(step * 2 * block, raw_ref.shape[3])
        weight_ref[2 * block * i : 2 * block * (i + step)] = piece

    arrived = recv_ref.at[pl.ds(0, count - 1)]
    pltpu.make_async_copy(arrived, arrived, recv_sem).wait()

    group = LANES // elems
    inside = lax.broadcasted_iota(jnp.int32, (2 * block, LANES), 1) // elems

    def place(q, carry):
        tiles = [recv_ref[q * group + i].astype(jnp.float32) for i in range(group)]
        pieces = []
        for f in range(frames):
            piece = None
            for i in range(group):
                shift = (elems * (i - f)) % LANES
                moved = pltpu.roll(tiles[i], shift, 1) if shift else tiles[i]
                piece = moved if piece is None else jnp.where(inside == i, moved, piece)
            pieces.append(piece)
        where = pl.multiple_of(q * LANES, LANES)
        picked_ref[:, pl.ds(where, LANES)] = jnp.concatenate(pieces, axis=0).astype(jnp.bfloat16)
        return carry

    steps = count // group
    if steps <= 8:
        for q in range(steps):
            place(q, 0)
    else:
        lax.fori_loop(0, steps, place, 0)
    product = lax.dot_general(
        picked_ref[...], weight_ref[...], NT, preferred_element_type=jnp.float32
    )
    at = lax.broadcasted_iota(jnp.int32, product.shape, 1)
    row = lax.broadcasted_iota(jnp.int32, product.shape, 0)
    product = jnp.where(at % block == row % block, product, 0.0)
    high, low = split(product)
    summed = jnp.dot(high, gather, preferred_element_type=jnp.float32) + jnp.dot(
        low, gather, preferred_element_type=jnp.float32
    )
    for f in range(frames):
        top = summed[2 * block * f : 2 * block * f + block]
        bottom = summed[2 * block * f + block : 2 * block * (f + 1)]
        real = top[:, :beams] - bottom[:, beams:]
        imag = bottom[:, :beams] + top[:, beams:]
        for s in range(block):
            beam_ref[0, pl.ds(s * frames + f, 1), :] = real[s : s + 1]
            beam_ref[1, pl.ds(s * frames + f, 1), :] = imag[s : s + 1]

    pltpu.make_async_copy(arrived, arrived, send_sem).wait()


def class_basis(chan):
    lanes = chan // RADIX
    b = np.arange(lanes)[:, None]
    d = np.arange(lanes)[None, :]
    out = []
    for c in range(RADIX):
        angle = 2.0 * np.pi / chan * (b * (c + RADIX * d) % chan)
        cos, sin = np.cos(angle) * chan**-0.5, np.sin(angle) * chan**-0.5
        out.append(np.block([[cos, -sin], [sin, cos]]))
    return jnp.asarray(np.stack(out), jnp.bfloat16)


def deliver_kernel(power_from, beam_from, power_to, beam_to, sems):
    copies = [
        pltpu.make_async_copy(power_from, power_to, sems.at[0]),
        pltpu.make_async_copy(beam_from, beam_to, sems.at[1]),
    ]
    for copy in copies:
        copy.start()
    for copy in copies:
        copy.wait()


def on_device(nelem, nchan, voltages, delays, prototype, subband_map, beam_weights):
    parts, elems, samples = voltages.shape
    taps, chan = prototype.shape
    beams, _, block, total = beam_weights.shape
    window = (FRAMES + taps - 1) * chan
    basis = class_basis(chan)
    count = nelem * nchan
    rows = 8
    chunks = parts * elems // rows
    out_shape = [
        jax.ShapeDtypeStruct((elems, chan), jnp.bfloat16),
        jax.ShapeDtypeStruct((2, block * FRAMES, beams), jnp.float32),
    ]
    power, beam = pl.pallas_call(
        functools.partial(main_kernel, nelem, nchan),
        in_specs=[pl.BlockSpec(memory_space=pltpu.HBM)] * 6,
        out_specs=[pl.BlockSpec(memory_space=pltpu.VMEM)] * 2,
        out_shape=[pltpu.VMEM(o.shape, o.dtype) for o in out_shape],
        scratch_shapes=[
            pltpu.SMEM(delays.shape, jnp.int32),
            pltpu.SMEM(subband_map.shape, jnp.int32),
            pltpu.VMEM((chunks, rows, samples), jnp.bfloat16),
            pltpu.VMEM((taps, chan), jnp.bfloat16),
            pltpu.VMEM(beam_weights.shape, jnp.bfloat16),
            pltpu.VMEM(basis.shape, jnp.bfloat16),
            pltpu.VMEM((2, rows, window), jnp.float32),
            pltpu.VMEM((taps, rows, chan), jnp.float32),
            pltpu.VMEM((parts, FRAMES, elems, chan), jnp.bfloat16),
            pltpu.VMEM((beams * 2 * block, total), jnp.bfloat16),
            pltpu.VMEM((nchan, 2 * block, FRAMES * elems), jnp.bfloat16),
            pltpu.VMEM((count, 2 * block, FRAMES * elems), jnp.bfloat16),
            pltpu.VMEM((2 * block * FRAMES, total), jnp.bfloat16),
            pltpu.SemaphoreType.DMA((5,)),
            pltpu.SemaphoreType.DMA((chunks,)),
            pltpu.SemaphoreType.DMA,
            pltpu.SemaphoreType.DMA,
        ],
        compiler_params=pltpu.CompilerParams(
            collective_id=0, has_side_effects=True, vmem_limit_bytes=66_400_000
        ),
    )(delays, subband_map, voltages, prototype, beam_weights, basis)
    return pl.pallas_call(
        deliver_kernel,
        in_specs=[pl.BlockSpec(memory_space=pl.ANY)] * 2,
        out_specs=[pl.BlockSpec(memory_space=pl.ANY)] * 2,
        out_shape=out_shape,
        scratch_shapes=[pltpu.SemaphoreType.DMA((2,))],
        compiler_params=pltpu.CompilerParams(vmem_limit_bytes=2**20),
    )(power, beam)


def solution(mesh):
    return jax.shard_map(
        functools.partial(on_device, mesh.shape["elem"], mesh.shape["chan"]),
        mesh=mesh,
        in_specs=(
            P(None, ("elem", "chan"), None),
            P(("elem", "chan")),
            P(),
            P(),
            P("elem", None, "chan", None),
        ),
        out_specs=(P(("elem", "chan"), None), P(None, "chan", "elem")),
        check_vma=False,
    )
```

profile of v0, /device:TPU:0, one launch (start us, length us, event | category | flops | bytes accessed | tf_op | source)
XLA Modules:
  0.0 14.4 jit_solution(10767765558349984862)
XLA Ops:
  0.6 13.1 %shard_map.77 = (bf16[32,1024]{1,0:T(8,128)(2,1)S(1)}, f32[2,16,64]{2,1,0:T(8,128)S(1)}) custom-call(s32[32]{0:T(128)} %delay_hbm.1, s32[16]{0:T(128)} %map_hbm.1, bf16[2,32,19584]{2,1,0:T(8,128)(2,1)} %volt_hbm.1, bf16[16,1024]{1,0:T(8,128)(2,1)} %proto_hbm.1, bf16[64,2,4,1024]{3,2,1,0:T(4,128)(2,1)} %weight_hbm.1, bf16[8,256,256]{2,1,0:T(8,128)(2,1)} %constant.2.clone.basis_hbm), custom_call_target="tpu_custom_call" | custom-call | tf_op jit(solution)/shard_map/pallas_call | solution.py:405
  13.8 0.7 %shard_map.78 = (bf16[32,1024]{1,0:T(8,128)(2,1)}, f32[2,16,64]{2,1,0:T(8,128)}) custom-call(bf16[32,1024]{1,0:T(8,128)(2,1)S(1)} %get-tuple-element.4.power_from, f32[2,16,64]{2,1,0:T(8,128)S(1)} %get-tuple-element.5.beam_from), custom_call_target="tpu_custom_call" | custom-call | tf_op jit(solution)/shard_map/pallas_call | solution.py:433
where the time goes:
time: 14.5 us; the launch traced here: 14.4 us
  Pallas kernels  13.8 us (95%)
  between operations  0.64 us (4%)
    pallas_call x1, Pallas kernels, on_device(): pl.pallas_call(functools.partial(main_kernel, nelem, nchan), in_specs=[pl...  13.1 us
    pallas_call x1, Pallas kernels, on_device(): pl.pallas_call(deliver_kernel, in_specs=[pl.BlockSpec(memory_space=pl.ANY...  0.65 us

commit v1 on v0

v1 whole, which is shorter than its diff:
```python
import functools
import math

import jax
import jax.numpy as jnp
import numpy as np
from jax import lax
from jax.experimental import pallas as pl
from jax.experimental.pallas import tpu as pltpu
from jax.sharding import PartitionSpec as P

FRAMES = 4
LANES = 128
ROWS = 8
RADIX = 8
LOGICAL = pl.DeviceIdType.LOGICAL
NT = (((1,), (1,)), ((), ()))
TN = (((0,), (0,)), ((), ()))


def cosine(turns, chan):
    y = jnp.abs((turns & (chan - 1)) - chan // 2) - chan // 4
    x = y.astype(jnp.float32) * (2.0 * math.pi / chan)
    s = x * x
    poly = 1.0 / 362880 - s * (1.0 / 39916800)
    poly = -1.0 / 5040 + s * poly
    poly = 1.0 / 120 + s * poly
    poly = -1.0 / 6 + s * poly
    return x + x * s * poly


def sine(turns, chan):
    return cosine(turns + 3 * (chan // 4), chan)


def eight_points(x):
    def add(a, b):
        return (a[0] + b[0], a[1] + b[1])

    def sub(a, b):
        return (a[0] - b[0], a[1] - b[1])

    def minus_i(a):
        return (a[1], -a[0])

    def four(v):
        a, b = add(v[0], v[2]), sub(v[0], v[2])
        c, d = add(v[1], v[3]), minus_i(sub(v[1], v[3]))
        return [add(a, c), add(b, d), sub(a, c), sub(b, d)]

    root = math.sqrt(0.5)
    even = four([add(x[a], x[a + 4]) for a in range(4)])
    d = [sub(x[a], x[a + 4]) for a in range(4)]
    d1 = ((d[1][0] + d[1][1]) * root, (d[1][1] - d[1][0]) * root)
    d3 = ((d[3][1] - d[3][0]) * root, (-d[3][0] - d[3][1]) * root)
    odd = four([d[0], d1, minus_i(d[2]), d3])
    out = []
    for e, o in zip(even, odd):
        out += [e, o]
    return out


def turn_plan(group, delay_ref):
    lane = lax.broadcasted_iota(jnp.int32, (ROWS, LANES), 1)
    sub = lax.broadcasted_iota(jnp.int32, (ROWS, LANES), 0)
    shift = jnp.zeros((ROWS, LANES), jnp.int32)
    for i in range(ROWS):
        shift = jnp.where(sub == i, delay_ref[group * ROWS + i], shift)
    return (lane - shift) & (LANES - 1), lane < shift


def turn_tap(t, slot, plan, base_ref, coef_ref):
    index, early = plan
    per = base_ref.shape[2] // LANES
    turned = [
        jnp.take_along_axis(
            base_ref[t, :, pl.ds(j * LANES, LANES)], index, axis=1, mode="promise_in_bounds"
        )
        for j in range(per)
    ]
    for j in range(per):
        coef_ref[slot, t, :, pl.ds(j * LANES, LANES)] = jnp.where(
            early, turned[(j - 1) % per], turned[j]
        )


def filter_column(group, part, chunk, j, slot, early, volt_ref, coef_ref, wave_ref):
    _, taps, _, chan = coef_ref.shape
    per = chan // LANES
    blocks = FRAMES + taps - 1
    held = [
        volt_ref[chunk, :, pl.ds((b * per + j) * LANES, LANES)].astype(jnp.float32)
        for b in range(blocks + (j == 0))
    ]
    if j == 0:
        held = [jnp.where(early, held[b + 1], held[b]) for b in range(blocks)]
    sums = [None] * FRAMES
    for t in range(taps):
        coef = coef_ref[slot, t, :, pl.ds(j * LANES, LANES)]
        for f in range(FRAMES):
            term = coef * held[f + t]
            sums[f] = term if t == 0 else sums[f] + term
    for f in range(0, FRAMES, 2):
        where = (group * FRAMES + f) * ROWS
        wave_ref[part, pl.ds(where, 2 * ROWS), pl.ds(j * LANES, LANES)] = jnp.concatenate(
            sums[f : f + 2], axis=0
        ).astype(jnp.bfloat16)


def main_kernel(
    nelem,
    nchan,
    gather,
    delay_hbm,
    map_hbm,
    volt_hbm,
    proto_hbm,
    weight_hbm,
    basis_hbm,
    power_ref,
    beam_ref,
    delay_ref,
    map_ref,
    volt_ref,
    proto_ref,
    raw_ref,
    basis_ref,
    base_ref,
    coef_ref,
    pick_ref,
    wave_ref,
    weight_ref,
    turned_ref,
    send_ref,
    recv_ref,
    local_sem,
    volt_sem,
    send_sem,
    recv_sem,
):
    parts, wave_rows, chan = wave_ref.shape
    chunks = volt_ref.shape[0]
    groups = chunks // parts
    elems = groups * ROWS
    taps = proto_ref.shape[0]
    per = chan // LANES
    count = nelem * nchan
    elem_at, chan_at = lax.axis_index("elem"), lax.axis_index("chan")
    me = elem_at * nchan + chan_at
    near_start = elem_at < nelem // 2
    barrier = pltpu.get_barrier_semaphore()

    def each_partner(act):
        def row(k, carry):
            first = jnp.where(near_start, nelem - 1 - k, k) * nchan
            for c in range(nchan):

                @pl.when(first + c != me)
                def _():
                    act(first + c, c)

            return carry

        if count <= 64:
            for k in range(nelem):
                row(k, 0)
        else:
            lax.fori_loop(0, nelem, row, 0)

    order = [(g, r) for g in [*range(1, groups), 0] for r in range(parts)]
    map_copy = pltpu.make_async_copy(map_hbm, map_ref, local_sem.at[0])
    proto_copy = pltpu.make_async_copy(proto_hbm, proto_ref, local_sem.at[1])
    delay_copy = pltpu.make_async_copy(delay_hbm, delay_ref, local_sem.at[2])
    basis_copy = pltpu.make_async_copy(basis_hbm, basis_ref, local_sem.at[3])
    weight_copy = pltpu.make_async_copy(weight_hbm, raw_ref, local_sem.at[4])
    ahead = volt_sem.shape[0]
    volt_copies = [
        pltpu.make_async_copy(
            volt_hbm.at[r, pl.ds(g * ROWS, ROWS)], volt_ref.at[k], volt_sem.at[k % ahead]
        )
        for k, (g, r) in enumerate(order)
    ]
    proto_copy.start()
    delay_copy.start()
    map_copy.start()
    for copy in volt_copies[:ahead]:
        copy.start()

    def greet(other, c):
        pl.semaphore_signal(barrier, inc=1, device_id=other, device_id_type=LOGICAL)

    each_partner(greet)

    proto_copy.wait()
    for t in range(taps):
        base_ref[t] = jnp.broadcast_to(
            proto_ref[pl.ds(t, 1), :].astype(jnp.float32), (ROWS, chan)
        )
    delay_copy.wait()
    plan = turn_plan(order[0][0], delay_ref)
    for t in range(taps):
        turn_tap(t, 0, plan, base_ref, coef_ref)

    map_copy.wait()
    subbands = map_ref.shape[0]
    block = subbands // nchan
    row = lax.broadcasted_iota(jnp.int32, (subbands, LANES), 0)
    lane = lax.broadcasted_iota(jnp.int32, (subbands, LANES), 1)
    wanted = jnp.zeros((subbands, LANES), jnp.int32)
    for s in range(subbands):
        wanted = jnp.where(row == s, map_ref[s], wanted)
    scale = chan**-0.5
    cos, sin = cosine(wanted * lane, chan) * scale, sine(wanted * lane, chan) * scale
    cos_step, sin_step = cosine(wanted * LANES, chan), sine(wanted * LANES, chan)
    for j in range(per):
        if j:
            cos, sin = cos * cos_step - sin * sin_step, sin * cos_step + cos * sin_step
        where = pl.ds(j * LANES, LANES)
        pick_ref[0, pl.ds(0, subbands), where] = cos.astype(jnp.bfloat16)
        pick_ref[0, pl.ds(subbands, subbands), where] = (-sin).astype(jnp.bfloat16)
        pick_ref[1, pl.ds(0, subbands), where] = sin.astype(jnp.bfloat16)
        pick_ref[1, pl.ds(subbands, subbands), where] = cos.astype(jnp.bfloat16)
    column = lax.broadcasted_iota(jnp.int32, (ROWS, LANES), 1)
    column = column // (FRAMES * ROWS) * ROWS + column % ROWS
    late = jnp.zeros((ROWS, LANES), jnp.int32)
    for e in range(elems):
        late = jnp.where(column == e, delay_ref[e], late)
    late = jnp.concatenate([late] * (subbands // ROWS), axis=0)
    cos_late, sin_late = cosine(wanted * late, chan), sine(wanted * late, chan)

    def arrive(k):
        volt_copies[k].wait()
        if k + ahead < chunks:
            volt_copies[k + ahead].start()
        elif k + ahead == chunks:
            basis_copy.start()
            weight_copy.start()

    span = FRAMES * ROWS
    inside = lane // span
    chosen = [None, None]
    for k, (g, r) in enumerate(order):
        arrive(k)
        slot = k // parts % 2
        if r == 0:
            early = plan[1]
            if k + parts < chunks:
                plan = turn_plan(order[k + parts][0], delay_ref)
        both = None
        for j in range(per):
            filter_column(g, r, k, j, slot, early, volt_ref, coef_ref, wave_ref)
            if k + parts < chunks:
                here = taps // parts
                for t in range(r * here + j * here // per, r * here + (j + 1) * here // per):
                    turn_tap(t, 1 - slot, plan, base_ref, coef_ref)
        if r == parts - 1:
            both = sum(
                lax.dot_general(
                    pick_ref[q],
                    wave_ref[q, pl.ds(g * span, span)],
                    NT,
                    preferred_element_type=jnp.float32,
                )
                for q in range(parts)
            )
            if span < LANES:
                both = jnp.concatenate(
                    [both, jnp.zeros((both.shape[0], LANES - span), jnp.float32)], axis=1
                )
            if g:
                both = pltpu.roll(both, g * span, 1)
            for i in range(2):
                piece = both[i * subbands : (i + 1) * subbands]
                chosen[i] = (
                    piece if chosen[i] is None else jnp.where(inside == g, piece, chosen[i])
                )
    real = chosen[0] * cos_late - chosen[1] * sin_late
    imag = chosen[1] * cos_late + chosen[0] * sin_late
    for c in range(nchan):
        part = slice(c * block, (c + 1) * block)
        send_ref[c] = jnp.concatenate([real[part], imag[part]], axis=0).astype(jnp.bfloat16)

    pl.semaphore_wait(barrier, count - 1)
    my_set = me // gather

    def send(other, c):
        pltpu.make_async_remote_copy(
            src_ref=send_ref.at[c],
            dst_ref=recv_ref.at[me],
            send_sem=send_sem,
            recv_sem=recv_sem.at[my_set],
            device_id=other,
            device_id_type=LOGICAL,
        ).start()

    each_partner(send)
    recv_ref[me] = send_ref[chan_at]

    lanes = chan // RADIX
    wave = [wave_ref[r] for r in range(2)]
    split_wave = [
        tuple(wave[r][:, a * lanes : (a + 1) * lanes].astype(jnp.float32) for r in range(2))
        for a in range(RADIX)
    ]
    classes = eight_points(split_wave)
    basis_copy.wait()
    powers = []
    for c in range(RADIX):
        mixed = jnp.concatenate(classes[c], axis=1).astype(jnp.bfloat16)
        spec = jnp.dot(mixed, basis_ref[c], preferred_element_type=jnp.float32)
        both = spec[:, :lanes] * spec[:, :lanes] + spec[:, lanes:] * spec[:, lanes:]
        totals = []
        for g in range(groups):
            tiles = [
                both[(g * FRAMES + f) * ROWS : (g * FRAMES + f + 1) * ROWS] for f in range(FRAMES)
            ]
            totals.append(sum(tiles[1:], tiles[0]))
        powers.append(jnp.concatenate(totals, axis=0) * (1.0 / FRAMES))
    wide = lanes // RADIX
    at = lax.broadcasted_iota(jnp.int32, (elems, lanes), 1)
    mixed = []
    for e in range(RADIX):
        piece = None
        for c in range(RADIX):
            shift = (wide * (c - e)) % lanes
            moved = pltpu.roll(powers[c], shift, 1) if shift else powers[c]
            piece = moved if piece is None else jnp.where(at // wide == c, moved, piece)
        mixed.append(piece)
    mixed = jnp.concatenate(mixed, axis=0).astype(jnp.bfloat16)
    down = lax.broadcasted_iota(jnp.int32, (lanes, lanes), 0)
    over = lax.broadcasted_iota(jnp.int32, (lanes, lanes), 1)
    back = (over == (down % wide) * RADIX + down // wide).astype(jnp.float32)
    final = jnp.dot(mixed, back.astype(jnp.bfloat16), preferred_element_type=jnp.float32)
    for e in range(RADIX):
        power_ref[:, e * lanes : (e + 1) * lanes] = final[e * elems : (e + 1) * elems].astype(
            jnp.bfloat16
        )

    beams = raw_ref.shape[0]
    weight_rows, total = weight_ref.shape
    wide_beams = turned_ref.shape[1] // block
    down = lax.broadcasted_iota(jnp.int32, (weight_rows, block * wide_beams), 0)
    over = lax.broadcasted_iota(jnp.int32, (weight_rows, block * wide_beams), 1)
    target = down % block * wide_beams + down // block % 2 * (wide_beams // 2)
    sort = (over == target + down // (2 * block)).astype(jnp.float32).astype(jnp.bfloat16)
    weight_copy.wait()
    step = min(8, beams)
    for i in range(0, beams, step):
        piece = raw_ref[i : i + step].reshape(step * 2 * block, raw_ref.shape[3])
        weight_ref[2 * block * i : 2 * block * (i + step)] = piece
    fan = LANES // elems

    def turn_weights(q, carry):
        depth = min(total, 8 * LANES)
        where = pl.multiple_of(q * depth, depth)
        turned = lax.dot_general(
            weight_ref[:, pl.ds(where, depth)], sort, TN, preferred_element_type=jnp.float32
        )
        for z in range(0, depth, LANES):
            tiles = [
                turned[z + (i * groups + g) * ROWS : z + (i * groups + g + 1) * ROWS]
                for g in range(groups)
                for i in range(fan)
            ]
            turned_ref[pl.ds(pl.multiple_of(where + z, LANES), LANES), :] = jnp.concatenate(
                tiles, axis=0
            ).astype(jnp.bfloat16)
        return carry

    if total <= 8 * LANES:
        turn_weights(0, 0)
    else:
        lax.fori_loop(0, total // (8 * LANES), turn_weights, 0)

    sets = count // gather
    place_at = lax.broadcasted_iota(jnp.int32, (2 * block, LANES), 1) // ROWS % fan
    low_row = lax.broadcasted_iota(jnp.int32, (2 * block, wide_beams), 0)

    def take(k, carry):
        which = jnp.where(near_start, k, sets - 1 - k)
        first = which * gather

        def arrived(n):
            some = recv_ref.at[pl.ds(0, n)]
            pltpu.make_async_copy(some, some, recv_sem.at[which]).wait()

        pl.when(which == my_set)(lambda: arrived(gather - 1))
        pl.when(which != my_set)(lambda: arrived(gather))
        pieces = [[] for _ in range(FRAMES)]
        for q in range(gather // fan):
            tiles = [recv_ref[first + q * fan + i].astype(jnp.float32) for i in range(fan)]
            for f in range(FRAMES):
                piece = None
                for i in range(fan):
                    shift = (ROWS * (i - f)) % LANES
                    moved = pltpu.roll(tiles[i], shift, 1) if shift else tiles[i]
                    piece = moved if piece is None else jnp.where(place_at == i, moved, piece)
                pieces[f].append(piece)
        picked = jnp.concatenate(
            [jnp.concatenate(p, axis=1) for p in pieces], axis=0
        ).astype(jnp.bfloat16)
        depth = gather * elems
        where = pl.multiple_of(which * depth, depth)
        product = jnp.dot(
            picked, turned_ref[pl.ds(where, depth), :], preferred_element_type=jnp.float32
        )
        out = []
        for f in range(FRAMES):
            tile = product[2 * block * f : 2 * block * (f + 1)]
            piece = tile[:, :wide_beams]
            for s in range(1, block):
                piece = jnp.where(
                    low_row % block == s, tile[:, s * wide_beams : (s + 1) * wide_beams], piece
                )
            out.append(piece if carry is None else carry[f] + piece)
        return tuple(out)

    if sets <= 8:
        sums = None
        for k in range(sets):
            sums = take(k, sums)
    else:
        zero = jnp.zeros((2 * block, wide_beams), jnp.float32)
        sums = lax.fori_loop(0, sets, take, (zero,) * FRAMES)
    for f in range(FRAMES):
        other = pltpu.roll(pltpu.roll(sums[f], wide_beams // 2, 1), block, 0)
        out = sums[f] + jnp.where(low_row < block, -other, other)
        for p in range(2):
            for s in range(block):
                at = p * block + s
                beam_ref[p, pl.ds(s * FRAMES + f, 1), :] = out[at : at + 1, :beams]

    sent = recv_ref.at[pl.ds(0, count - 1)]
    pltpu.make_async_copy(sent, sent, send_sem).wait()


def class_basis(chan):
    lanes = chan // RADIX
    b = np.arange(lanes)[:, None]
    d = np.arange(lanes)[None, :]
    out = []
    for c in range(RADIX):
        angle = 2.0 * np.pi / chan * (b * (c + RADIX * d) % chan)
        cos, sin = np.cos(angle) * chan**-0.5, np.sin(angle) * chan**-0.5
        out.append(np.block([[cos, -sin], [sin, cos]]))
    return jnp.asarray(np.stack(out), jnp.bfloat16)


def deliver_kernel(power_from, beam_from, power_to, beam_to, sems):
    copies = [
        pltpu.make_async_copy(power_from, power_to, sems.at[0]),
        pltpu.make_async_copy(beam_from, beam_to, sems.at[1]),
    ]
    for copy in copies:
        copy.start()
    for copy in copies:
        copy.wait()


def on_device(nelem, nchan, voltages, delays, prototype, subband_map, beam_weights):
    parts, elems, samples = voltages.shape
    taps, chan = prototype.shape
    beams, _, block, total = beam_weights.shape
    basis = class_basis(chan)
    count = nelem * nchan
    chunks = parts * elems // ROWS
    gather = 8
    wide_beams = max(LANES, 2 * beams)
    out_shape = [
        jax.ShapeDtypeStruct((elems, chan), jnp.bfloat16),
        jax.ShapeDtypeStruct((2, block * FRAMES, beams), jnp.float32),
    ]
    power, beam = pl.pallas_call(
        functools.partial(main_kernel, nelem, nchan, gather),
        in_specs=[pl.BlockSpec(memory_space=pltpu.HBM)] * 6,
        out_specs=[pl.BlockSpec(memory_space=pltpu.VMEM)] * 2,
        out_shape=[pltpu.VMEM(o.shape, o.dtype) for o in out_shape],
        scratch_shapes=[
            pltpu.SMEM(delays.shape, jnp.int32),
            pltpu.SMEM(subband_map.shape, jnp.int32),
            pltpu.VMEM((chunks, ROWS, samples), jnp.bfloat16),
            pltpu.VMEM((taps, chan), jnp.bfloat16),
            pltpu.VMEM(beam_weights.shape, jnp.bfloat16),
            pltpu.VMEM(basis.shape, jnp.bfloat16),
            pltpu.VMEM((taps, ROWS, chan), jnp.float32),
            pltpu.VMEM((2, taps, ROWS, chan), jnp.float32),
            pltpu.VMEM((2, 2 * subband_map.shape[0], chan), jnp.bfloat16),
            pltpu.VMEM((parts, FRAMES * elems, chan), jnp.bfloat16),
            pltpu.VMEM((beams * 2 * block, total), jnp.bfloat16),
            pltpu.VMEM((total, block * wide_beams), jnp.bfloat16),
            pltpu.VMEM((nchan, 2 * block, FRAMES * elems), jnp.bfloat16),
            pltpu.VMEM((count, 2 * block, FRAMES * elems), jnp.bfloat16),
            pltpu.SemaphoreType.DMA((5,)),
            pltpu.SemaphoreType.DMA((4,)),
            pltpu.SemaphoreType.DMA,
            pltpu.SemaphoreType.DMA((count // gather,)),
        ],
        compiler_params=pltpu.CompilerParams(
            collective_id=0, has_side_effects=True, vmem_limit_bytes=66_400_000
        ),
    )(delays, subband_map, voltages, prototype, beam_weights, basis)
    return pl.pallas_call(
        deliver_kernel,
        in_specs=[pl.BlockSpec(memory_space=pl.ANY)] * 2,
        out_specs=[pl.BlockSpec(memory_space=pl.ANY)] * 2,
        out_shape=out_shape,
        scratch_shapes=[pltpu.SemaphoreType.DMA((2,))],
        compiler_params=pltpu.CompilerParams(vmem_limit_bytes=2**20),
    )(power, beam)


def solution(mesh):
    return jax.shard_map(
        functools.partial(on_device, mesh.shape["elem"], mesh.shape["chan"]),
        mesh=mesh,
        in_specs=(
            P(None, ("elem", "chan"), None),
            P(("elem", "chan")),
            P(),
            P(),
            P("elem", None, "chan", None),
        ),
        out_specs=(P(("elem", "chan"), None), P(None, "chan", "elem")),
        check_vma=False,
    )
```

time: 14.5 us -> 14.2 us (0.979)
  Pallas kernels: 13.8 us -> 13.4 us
    pallas_call x1, Pallas kernels: 13.1 us -> 12.8 us  [on_device(): pl.pallas_call(functools.partial(main_kernel, nelem, nchan, gather), in_s...]
where the time goes in v1:
time: 14.2 us; the launch traced here: 14.1 us
  Pallas kernels  13.4 us (94%)
  between operations  0.64 us (5%)
    pallas_call x1, Pallas kernels, on_device(): pl.pallas_call(functools.partial(main_kernel, nelem, nchan, gather), in_s...  12.8 us
    pallas_call x1, Pallas kernels, on_device(): pl.pallas_call(deliver_kernel, in_specs=[pl.BlockSpec(memory_space=pl.ANY...  0.65 us

profile of v1, /device:TPU:0, one launch (start us, length us, event | category | flops | bytes accessed | tf_op | source)
XLA Modules:
  0.0 14.1 jit_solution(15754259412925342015)
XLA Ops:
  0.6 12.8 %shard_map.77 = (bf16[32,1024]{1,0:T(8,128)(2,1)S(1)}, f32[2,16,64]{2,1,0:T(8,128)S(1)}) custom-call(s32[32]{0:T(128)} %delay_hbm.1, s32[16]{0:T(128)} %map_hbm.1, bf16[2,32,19584]{2,1,0:T(8,128)(2,1)} %volt_hbm.1, bf16[16,1024]{1,0:T(8,128)(2,1)} %proto_hbm.1, bf16[64,2,4,1024]{3,2,1,0:T(4,128)(2,1)} %weight_hbm.1, bf16[8,256,256]{2,1,0:T(8,128)(2,1)} %constant.2.clone.basis_hbm), custom_call_target="tpu_custom_call" | custom-call | tf_op jit(solution)/shard_map/pallas_call | solution.py:473
  13.4 0.7 %shard_map.78 = (bf16[32,1024]{1,0:T(8,128)(2,1)}, f32[2,16,64]{2,1,0:T(8,128)}) custom-call(bf16[32,1024]{1,0:T(8,128)(2,1)S(1)} %get-tuple-element.4.power_from, f32[2,16,64]{2,1,0:T(8,128)S(1)} %get-tuple-element.5.beam_from), custom_call_target="tpu_custom_call" | custom-call | tf_op jit(solution)/shard_map/pallas_call | solution.py:502

commit v2 on v1

--- a/solution.py
+++ b/solution.py
@@ -69,42 +69,55 @@
     return (lane - shift) & (LANES - 1), lane < shift
 
 
-def turn_tap(t, slot, plan, base_ref, coef_ref):
+def turn_pair(pair, slot, plan, proto_ref, turned_ref, coef_ref):
     index, early = plan
-    per = base_ref.shape[2] // LANES
-    turned = [
-        jnp.take_along_axis(
-            base_ref[t, :, pl.ds(j * LANES, LANES)], index, axis=1, mode="promise_in_bounds"
-        )
-        for j in range(per)
-    ]
-    for j in range(per):
-        coef_ref[slot, t, :, pl.ds(j * LANES, LANES)] = jnp.where(
-            early, turned[(j - 1) % per], turned[j]
-        )
-
-
-def filter_column(group, part, chunk, j, slot, early, volt_ref, coef_ref, wave_ref):
+    taps, chan = proto_ref.shape
+    per = chan // LANES
+    first, last = 2 * pair, min(2 * pair + 2, per - 1)
+    fresh = [*range(first, last), per - 1] if pair == 0 else range(first, last)
+    for t in range(taps):
+        for j in fresh:
+            where = pl.ds(j * LANES, LANES)
+            value = jnp.broadcast_to(proto_ref[pl.ds(t, 1), where], (ROWS, LANES))
+            turned_ref[t, :, where] = jnp.take_along_axis(
+                value, index, axis=1, mode="promise_in_bounds"
+            )
+        near = [
+            turned_ref[t, :, pl.ds((first + i) % per * LANES, LANES)] for i in (-1, 0, 1)
+        ]
+        coef_ref[slot, t, :, pl.ds(first * LANES, 2 * LANES)] = jnp.concatenate(
+            [jnp.where(early, near[0], near[1]), jnp.where(early, near[1], near[2])], axis=1
+        ).astype(jnp.bfloat16)
+
+
+def filter_pair(group, part, chunk, pair, slot, early, volt_ref, coef_ref, wave_ref):
     _, taps, _, chan = coef_ref.shape
-    per = chan // LANES
     blocks = FRAMES + taps - 1
-    held = [
-        volt_ref[chunk, :, pl.ds((b * per + j) * LANES, LANES)].astype(jnp.float32)
-        for b in range(blocks + (j == 0))
-    ]
-    if j == 0:
-        held = [jnp.where(early, held[b + 1], held[b]) for b in range(blocks)]
-    sums = [None] * FRAMES
+    wide = 2 * LANES
+
+    def column(b, size):
+        return volt_ref[chunk, :, pl.ds(b * chan + pair * wide, size)]
+
+    held = [column(b, wide) for b in range(blocks)]
+    if pair == 0:
+        last = jnp.concatenate([column(blocks, LANES), held[-1][:, LANES:]], axis=1)
+        held = [
+            jnp.where(early, nxt, now) for now, nxt in zip(held, [*held[1:], last])
+        ]
+    stacks = [[] for _ in range(FRAMES)]
     for t in range(taps):
-        coef = coef_ref[slot, t, :, pl.ds(j * LANES, LANES)]
+        coef = coef_ref[slot, t, :, pl.ds(pair * wide, wide)]
         for f in range(FRAMES):
-            term = coef * held[f + t]
-            sums[f] = term if t == 0 else sums[f] + term
-    for f in range(0, FRAMES, 2):
-        where = (group * FRAMES + f) * ROWS
-        wave_ref[part, pl.ds(where, 2 * ROWS), pl.ds(j * LANES, LANES)] = jnp.concatenate(
-            sums[f : f + 2], axis=0
-        ).astype(jnp.bfloat16)
+            level, term = 0, coef * held[f + t]
+            while stacks[f] and stacks[f][-1][0] == level:
+                level, term = level + 1, stacks[f].pop()[1] + term
+            stacks[f].append((level, term))
+    for f in range(FRAMES):
+        total = stacks[f].pop()[1]
+        while stacks[f]:
+            total = stacks[f].pop()[1] + total
+        where = pl.ds((group * FRAMES + f) * ROWS, ROWS)
+        wave_ref[part, where, pl.ds(pair * wide, wide)] = total
 
 
 def main_kernel(
@@ -125,7 +138,8 @@
     proto_ref,
     raw_ref,
     basis_ref,
-    base_ref,
+    wide_ref,
+    spun_ref,
     coef_ref,
     pick_ref,
     wave_ref,
@@ -191,16 +205,6 @@
 
     each_partner(greet)
 
-    proto_copy.wait()
-    for t in range(taps):
-        base_ref[t] = jnp.broadcast_to(
-            proto_ref[pl.ds(t, 1), :].astype(jnp.float32), (ROWS, chan)
-        )
-    delay_copy.wait()
-    plan = turn_plan(order[0][0], delay_ref)
-    for t in range(taps):
-        turn_tap(t, 0, plan, base_ref, coef_ref)
-
     map_copy.wait()
     subbands = map_ref.shape[0]
     block = subbands // nchan
@@ -220,6 +224,7 @@
         pick_ref[0, pl.ds(subbands, subbands), where] = (-sin).astype(jnp.bfloat16)
         pick_ref[1, pl.ds(0, subbands), where] = sin.astype(jnp.bfloat16)
         pick_ref[1, pl.ds(subbands, subbands), where] = cos.astype(jnp.bfloat16)
+    delay_copy.wait()
     column = lax.broadcasted_iota(jnp.int32, (ROWS, LANES), 1)
     column = column // (FRAMES * ROWS) * ROWS + column % ROWS
     late = jnp.zeros((ROWS, LANES), jnp.int32)
@@ -232,48 +237,65 @@
         volt_copies[k].wait()
         if k + ahead < chunks:
             volt_copies[k + ahead].start()
-        elif k + ahead == chunks:
+        if k == parts:
             basis_copy.start()
             weight_copy.start()
 
     span = FRAMES * ROWS
     inside = lane // span
     chosen = [None, None]
+    products = {}
+
+    def pick(g, r):
+        products[g, r] = lax.dot_general(
+            pick_ref[r],
+            wave_ref[r, pl.ds(g * span, span)],
+            NT,
+            preferred_element_type=jnp.float32,
+        )
+
+    def join(g):
+        both = sum(products[g, r] for r in range(parts))
+        if span < LANES:
+            both = jnp.concatenate(
+                [both, jnp.zeros((both.shape[0], LANES - span), jnp.float32)], axis=1
+            )
+        if g:
+            both = pltpu.roll(both, g * span, 1)
+        for i in range(2):
+            piece = both[i * subbands : (i + 1) * subbands]
+            chosen[i] = piece if chosen[i] is None else jnp.where(inside == g, piece, chosen[i])
+
+    proto_copy.wait()
+    wide_ref[...] = proto_ref[...].astype(jnp.float32)
+    pairs = per // 2
+    plan = turn_plan(order[0][0], delay_ref)
+    turn_pair(0, 0, plan, wide_ref, spun_ref, coef_ref)
+    todo = [[] for _ in order]
+    for n in range(groups):
+        for p in range(n == 0, pairs):
+            ahead_by = parts if n > 1 else 1
+            spread = p * ahead_by // pairs
+            todo[max(0, n * parts - ahead_by) + spread].append((n, p))
+    plans = {0: plan}
     for k, (g, r) in enumerate(order):
         arrive(k)
-        slot = k // parts % 2
-        if r == 0:
-            early = plan[1]
-            if k + parts < chunks:
-                plan = turn_plan(order[k + parts][0], delay_ref)
-        both = None
-        for j in range(per):
-            filter_column(g, r, k, j, slot, early, volt_ref, coef_ref, wave_ref)
-            if k + parts < chunks:
-                here = taps // parts
-                for t in range(r * here + j * here // per, r * here + (j + 1) * here // per):
-                    turn_tap(t, 1 - slot, plan, base_ref, coef_ref)
-        if r == parts - 1:
-            both = sum(
-                lax.dot_general(
-                    pick_ref[q],
-                    wave_ref[q, pl.ds(g * span, span)],
-                    NT,
-                    preferred_element_type=jnp.float32,
-                )
-                for q in range(parts)
-            )
-            if span < LANES:
-                both = jnp.concatenate(
-                    [both, jnp.zeros((both.shape[0], LANES - span), jnp.float32)], axis=1
-                )
-            if g:
-                both = pltpu.roll(both, g * span, 1)
-            for i in range(2):
-                piece = both[i * subbands : (i + 1) * subbands]
-                chosen[i] = (
-                    piece if chosen[i] is None else jnp.where(inside == g, piece, chosen[i])
-                )
+        n = k // parts
+        early = plans[n][1].astype(jnp.int32)
+        early = jnp.concatenate([early, jnp.zeros_like(early)], axis=1) != 0
+        if k:
+            pick(*order[k - 1])
+        if k >= parts and r == 1:
+            join(order[k - parts][0])
+        for p in range(pairs):
+            filter_pair(g, r, k, p, n % 2, early, volt_ref, coef_ref, wave_ref)
+            if todo[k]:
+                unit, q = todo[k].pop(0)
+                if unit not in plans:
+                    plans[unit] = turn_plan(order[unit * parts][0], delay_ref)
+                turn_pair(q, unit % 2, plans[unit], wide_ref, spun_ref, coef_ref)
+    pick(*order[-1])
+    join(order[-1][0])
     real = chosen[0] * cos_late - chosen[1] * sin_late
     imag = chosen[1] * cos_late + chosen[0] * sin_late
     for c in range(nchan):
@@ -482,8 +504,9 @@
             pltpu.VMEM((taps, chan), jnp.bfloat16),
             pltpu.VMEM(beam_weights.shape, jnp.bfloat16),
             pltpu.VMEM(basis.shape, jnp.bfloat16),
+            pltpu.VMEM((taps, chan), jnp.float32),
             pltpu.VMEM((taps, ROWS, chan), jnp.float32),
-            pltpu.VMEM((2, taps, ROWS, chan), jnp.float32),
+            pltpu.VMEM((2, taps, ROWS, chan), jnp.bfloat16),
             pltpu.VMEM((2, 2 * subband_map.shape[0], chan), jnp.bfloat16),
             pltpu.VMEM((parts, FRAMES * elems, chan), jnp.bfloat16),
             pltpu.VMEM((beams * 2 * block, total), jnp.bfloat16),
@@ -491,7 +514,7 @@
             pltpu.VMEM((nchan, 2 * block, FRAMES * elems), jnp.bfloat16),
             pltpu.VMEM((count, 2 * block, FRAMES * elems), jnp.bfloat16),
             pltpu.SemaphoreType.DMA((5,)),
-            pltpu.SemaphoreType.DMA((4,)),
+            pltpu.SemaphoreType.DMA((chunks,)),
             pltpu.SemaphoreType.DMA,
             pltpu.SemaphoreType.DMA((count // gather,)),
         ],

time: 14.2 us -> 13.4 us (0.944)
  Pallas kernels: 13.4 us -> 12.7 us
    pallas_call x1, Pallas kernels: 12.8 us -> 12 us  [on_device(): pl.pallas_call(functools.partial(main_kernel, nelem, nchan, gather), in_s...]
where the time goes in v2:
time: 13.4 us; the launch traced here: 13.3 us
  Pallas kernels  12.7 us (95%)
  between operations  0.64 us (5%)
    pallas_call x1, Pallas kernels, on_device(): pl.pallas_call(functools.partial(main_kernel, nelem, nchan, gather), in_s...  12 us
    pallas_call x1, Pallas kernels, on_device(): pl.pallas_call(deliver_kernel, in_specs=[pl.BlockSpec(memory_space=pl.ANY...  0.65 us

profile of v2, /device:TPU:0, one launch (start us, length us, event | category | flops | bytes accessed | tf_op | source)
XLA Modules:
  0.0 13.3 jit_solution(16091986855765643463)
XLA Ops:
  0.6 12.0 %shard_map.77 = (bf16[32,1024]{1,0:T(8,128)(2,1)S(1)}, f32[2,16,64]{2,1,0:T(8,128)S(1)}) custom-call(s32[32]{0:T(128)} %delay_hbm.1, s32[16]{0:T(128)} %map_hbm.1, bf16[2,32,19584]{2,1,0:T(8,128)(2,1)} %volt_hbm.1, bf16[16,1024]{1,0:T(8,128)(2,1)} %proto_hbm.1, bf16[64,2,4,1024]{3,2,1,0:T(4,128)(2,1)} %weight_hbm.1, bf16[8,256,256]{2,1,0:T(8,128)(2,1)} %constant.2.clone.basis_hbm), custom_call_target="tpu_custom_call" | custom-call | tf_op jit(solution)/shard_map/pallas_call | solution.py:495
  12.6 0.7 %shard_map.78 = (bf16[32,1024]{1,0:T(8,128)(2,1)}, f32[2,16,64]{2,1,0:T(8,128)}) custom-call(bf16[32,1024]{1,0:T(8,128)(2,1)S(1)} %get-tuple-element.4.power_from, f32[2,16,64]{2,1,0:T(8,128)S(1)} %get-tuple-element.5.beam_from), custom_call_target="tpu_custom_call" | custom-call | tf_op jit(solution)/shard_map/pallas_call | solution.py:525

commit v3 on v2

--- a/solution.py
+++ b/solution.py
@@ -96,7 +96,7 @@
     wide = 2 * LANES
 
     def column(b, size):
-        return volt_ref[chunk, :, pl.ds(b * chan + pair * wide, size)]
+        return volt_ref[chunk, part, :, pl.ds(b * chan + pair * wide, size)]
 
     held = [column(b, wide) for b in range(blocks)]
     if pair == 0:
@@ -147,14 +147,11 @@
     turned_ref,
     send_ref,
     recv_ref,
-    local_sem,
-    volt_sem,
     send_sem,
     recv_sem,
 ):
     parts, wave_rows, chan = wave_ref.shape
-    chunks = volt_ref.shape[0]
-    groups = chunks // parts
+    groups = volt_ref.shape[0]
     elems = groups * ROWS
     taps = proto_ref.shape[0]
     per = chan // LANES
@@ -181,218 +178,224 @@
         else:
             lax.fori_loop(0, nelem, row, 0)
 
-    order = [(g, r) for g in [*range(1, groups), 0] for r in range(parts)]
-    map_copy = pltpu.make_async_copy(map_hbm, map_ref, local_sem.at[0])
-    proto_copy = pltpu.make_async_copy(proto_hbm, proto_ref, local_sem.at[1])
-    delay_copy = pltpu.make_async_copy(delay_hbm, delay_ref, local_sem.at[2])
-    basis_copy = pltpu.make_async_copy(basis_hbm, basis_ref, local_sem.at[3])
-    weight_copy = pltpu.make_async_copy(weight_hbm, raw_ref, local_sem.at[4])
-    ahead = volt_sem.shape[0]
-    volt_copies = [
-        pltpu.make_async_copy(
-            volt_hbm.at[r, pl.ds(g * ROWS, ROWS)], volt_ref.at[k], volt_sem.at[k % ahead]
-        )
-        for k, (g, r) in enumerate(order)
-    ]
-    proto_copy.start()
-    delay_copy.start()
-    map_copy.start()
-    for copy in volt_copies[:ahead]:
-        copy.start()
-
-    def greet(other, c):
-        pl.semaphore_signal(barrier, inc=1, device_id=other, device_id_type=LOGICAL)
-
-    each_partner(greet)
-
-    map_copy.wait()
     subbands = map_ref.shape[0]
     block = subbands // nchan
-    row = lax.broadcasted_iota(jnp.int32, (subbands, LANES), 0)
-    lane = lax.broadcasted_iota(jnp.int32, (subbands, LANES), 1)
-    wanted = jnp.zeros((subbands, LANES), jnp.int32)
-    for s in range(subbands):
-        wanted = jnp.where(row == s, map_ref[s], wanted)
-    scale = chan**-0.5
-    cos, sin = cosine(wanted * lane, chan) * scale, sine(wanted * lane, chan) * scale
-    cos_step, sin_step = cosine(wanted * LANES, chan), sine(wanted * LANES, chan)
-    for j in range(per):
-        if j:
-            cos, sin = cos * cos_step - sin * sin_step, sin * cos_step + cos * sin_step
-        where = pl.ds(j * LANES, LANES)
-        pick_ref[0, pl.ds(0, subbands), where] = cos.astype(jnp.bfloat16)
-        pick_ref[0, pl.ds(subbands, subbands), where] = (-sin).astype(jnp.bfloat16)
-        pick_ref[1, pl.ds(0, subbands), where] = sin.astype(jnp.bfloat16)
-        pick_ref[1, pl.ds(subbands, subbands), where] = cos.astype(jnp.bfloat16)
-    delay_copy.wait()
-    column = lax.broadcasted_iota(jnp.int32, (ROWS, LANES), 1)
-    column = column // (FRAMES * ROWS) * ROWS + column % ROWS
-    late = jnp.zeros((ROWS, LANES), jnp.int32)
-    for e in range(elems):
-        late = jnp.where(column == e, delay_ref[e], late)
-    late = jnp.concatenate([late] * (subbands // ROWS), axis=0)
-    cos_late, sin_late = cosine(wanted * late, chan), sine(wanted * late, chan)
-
-    def arrive(k):
-        volt_copies[k].wait()
-        if k + ahead < chunks:
-            volt_copies[k + ahead].start()
-        if k == parts:
-            basis_copy.start()
-            weight_copy.start()
-
-    span = FRAMES * ROWS
-    inside = lane // span
-    chosen = [None, None]
-    products = {}
-
-    def pick(g, r):
-        products[g, r] = lax.dot_general(
-            pick_ref[r],
-            wave_ref[r, pl.ds(g * span, span)],
-            NT,
-            preferred_element_type=jnp.float32,
-        )
-
-    def join(g):
-        both = sum(products[g, r] for r in range(parts))
-        if span < LANES:
-            both = jnp.concatenate(
-                [both, jnp.zeros((both.shape[0], LANES - span), jnp.float32)], axis=1
-            )
-        if g:
-            both = pltpu.roll(both, g * span, 1)
-        for i in range(2):
-            piece = both[i * subbands : (i + 1) * subbands]
-            chosen[i] = piece if chosen[i] is None else jnp.where(inside == g, piece, chosen[i])
-
-    proto_copy.wait()
-    wide_ref[...] = proto_ref[...].astype(jnp.float32)
-    pairs = per // 2
-    plan = turn_plan(order[0][0], delay_ref)
-    turn_pair(0, 0, plan, wide_ref, spun_ref, coef_ref)
-    todo = [[] for _ in order]
-    for n in range(groups):
-        for p in range(n == 0, pairs):
-            ahead_by = parts if n > 1 else 1
-            spread = p * ahead_by // pairs
-            todo[max(0, n * parts - ahead_by) + spread].append((n, p))
-    plans = {0: plan}
-    for k, (g, r) in enumerate(order):
-        arrive(k)
-        n = k // parts
-        early = plans[n][1].astype(jnp.int32)
-        early = jnp.concatenate([early, jnp.zeros_like(early)], axis=1) != 0
-        if k:
-            pick(*order[k - 1])
-        if k >= parts and r == 1:
-            join(order[k - parts][0])
-        for p in range(pairs):
-            filter_pair(g, r, k, p, n % 2, early, volt_ref, coef_ref, wave_ref)
-            if todo[k]:
-                unit, q = todo[k].pop(0)
-                if unit not in plans:
-                    plans[unit] = turn_plan(order[unit * parts][0], delay_ref)
-                turn_pair(q, unit % 2, plans[unit], wide_ref, spun_ref, coef_ref)
-    pick(*order[-1])
-    join(order[-1][0])
-    real = chosen[0] * cos_late - chosen[1] * sin_late
-    imag = chosen[1] * cos_late + chosen[0] * sin_late
-    for c in range(nchan):
-        part = slice(c * block, (c + 1) * block)
-        send_ref[c] = jnp.concatenate([real[part], imag[part]], axis=0).astype(jnp.bfloat16)
-
-    pl.semaphore_wait(barrier, count - 1)
     my_set = me // gather
-
-    def send(other, c):
-        pltpu.make_async_remote_copy(
-            src_ref=send_ref.at[c],
-            dst_ref=recv_ref.at[me],
-            send_sem=send_sem,
-            recv_sem=recv_sem.at[my_set],
-            device_id=other,
-            device_id_type=LOGICAL,
-        ).start()
-
-    each_partner(send)
-    recv_ref[me] = send_ref[chan_at]
-
-    lanes = chan // RADIX
-    wave = [wave_ref[r] for r in range(2)]
-    split_wave = [
-        tuple(wave[r][:, a * lanes : (a + 1) * lanes].astype(jnp.float32) for r in range(2))
-        for a in range(RADIX)
-    ]
-    classes = eight_points(split_wave)
-    basis_copy.wait()
-    powers = []
-    for c in range(RADIX):
-        mixed = jnp.concatenate(classes[c], axis=1).astype(jnp.bfloat16)
-        spec = jnp.dot(mixed, basis_ref[c], preferred_element_type=jnp.float32)
-        both = spec[:, :lanes] * spec[:, :lanes] + spec[:, lanes:] * spec[:, lanes:]
-        totals = []
-        for g in range(groups):
-            tiles = [
-                both[(g * FRAMES + f) * ROWS : (g * FRAMES + f + 1) * ROWS] for f in range(FRAMES)
-            ]
-            totals.append(sum(tiles[1:], tiles[0]))
-        powers.append(jnp.concatenate(totals, axis=0) * (1.0 / FRAMES))
-    wide = lanes // RADIX
-    at = lax.broadcasted_iota(jnp.int32, (elems, lanes), 1)
-    mixed = []
-    for e in range(RADIX):
-        piece = None
-        for c in range(RADIX):
-            shift = (wide * (c - e)) % lanes
-            moved = pltpu.roll(powers[c], shift, 1) if shift else powers[c]
-            piece = moved if piece is None else jnp.where(at // wide == c, moved, piece)
-        mixed.append(piece)
-    mixed = jnp.concatenate(mixed, axis=0).astype(jnp.bfloat16)
-    down = lax.broadcasted_iota(jnp.int32, (lanes, lanes), 0)
-    over = lax.broadcasted_iota(jnp.int32, (lanes, lanes), 1)
-    back = (over == (down % wide) * RADIX + down // wide).astype(jnp.float32)
-    final = jnp.dot(mixed, back.astype(jnp.bfloat16), preferred_element_type=jnp.float32)
-    for e in range(RADIX):
-        power_ref[:, e * lanes : (e + 1) * lanes] = final[e * elems : (e + 1) * elems].astype(
-            jnp.bfloat16
-        )
-
     beams = raw_ref.shape[0]
     weight_rows, total = weight_ref.shape
     wide_beams = turned_ref.shape[1] // block
-    down = lax.broadcasted_iota(jnp.int32, (weight_rows, block * wide_beams), 0)
-    over = lax.broadcasted_iota(jnp.int32, (weight_rows, block * wide_beams), 1)
-    target = down % block * wide_beams + down // block % 2 * (wide_beams // 2)
-    sort = (over == target + down // (2 * block)).astype(jnp.float32).astype(jnp.bfloat16)
-    weight_copy.wait()
-    step = min(8, beams)
-    for i in range(0, beams, step):
-        piece = raw_ref[i : i + step].reshape(step * 2 * block, raw_ref.shape[3])
-        weight_ref[2 * block * i : 2 * block * (i + step)] = piece
     fan = LANES // elems
 
-    def turn_weights(q, carry):
-        depth = min(total, 8 * LANES)
-        where = pl.multiple_of(q * depth, depth)
-        turned = lax.dot_general(
-            weight_ref[:, pl.ds(where, depth)], sort, TN, preferred_element_type=jnp.float32
-        )
-        for z in range(0, depth, LANES):
-            tiles = [
-                turned[z + (i * groups + g) * ROWS : z + (i * groups + g + 1) * ROWS]
-                for g in range(groups)
-                for i in range(fan)
-            ]
-            turned_ref[pl.ds(pl.multiple_of(where + z, LANES), LANES), :] = jnp.concatenate(
-                tiles, axis=0
-            ).astype(jnp.bfloat16)
-        return carry
-
-    if total <= 8 * LANES:
-        turn_weights(0, 0)
-    else:
-        lax.fori_loop(0, total // (8 * LANES), turn_weights, 0)
+    def front(local_sem, volt_sem):
+        order = [*range(1, groups), 0]
+        map_copy = pltpu.make_async_copy(map_hbm, map_ref, local_sem.at[0])
+        proto_copy = pltpu.make_async_copy(proto_hbm, proto_ref, local_sem.at[1])
+        delay_copy = pltpu.make_async_copy(delay_hbm, delay_ref, local_sem.at[2])
+        basis_copy = pltpu.make_async_copy(basis_hbm, basis_ref, local_sem.at[3])
+        weight_copy = pltpu.make_async_copy(weight_hbm, raw_ref, local_sem.at[4])
+        volt_copies = [
+            pltpu.make_async_copy(
+                volt_hbm.at[r, pl.ds(order[0] * ROWS, ROWS)], volt_ref.at[0, r], volt_sem.at[r]
+            )
+            for r in range(parts)
+        ]
+        for k, g in enumerate(order[1:]):
+            volt_copies.append(
+                pltpu.make_async_copy(
+                    volt_hbm.at[:, pl.ds(g * ROWS, ROWS)],
+                    volt_ref.at[k + 1],
+                    volt_sem.at[k + parts],
+                )
+            )
+        proto_copy.start()
+        delay_copy.start()
+        map_copy.start()
+        for copy in volt_copies[:parts]:
+            copy.start()
+
+        def greet(other, c):
+            pl.semaphore_signal(barrier, inc=1, device_id=other, device_id_type=LOGICAL)
+
+        each_partner(greet)
+        for copy in volt_copies[parts:]:
+            copy.start()
+
+        map_copy.wait()
+        delay_copy.wait()
+        proto_copy.wait()
+        wide_ref[...] = proto_ref[...].astype(jnp.float32)
+        pairs = per // 2
+        plans = [turn_plan(order[0], delay_ref)]
+        turn_pair(0, 0, plans[0], wide_ref, spun_ref, coef_ref)
+        row = lax.broadcasted_iota(jnp.int32, (subbands, LANES), 0)
+        lane = lax.broadcasted_iota(jnp.int32, (subbands, LANES), 1)
+        wanted = jnp.zeros((subbands, LANES), jnp.int32)
+        for s in range(subbands):
+            wanted = jnp.where(row == s, map_ref[s], wanted)
+        scale = chan**-0.5
+        cos, sin = cosine(wanted * lane, chan) * scale, sine(wanted * lane, chan) * scale
+        cos_step, sin_step = cosine(wanted * LANES, chan), sine(wanted * LANES, chan)
+        for j in range(per):
+            if j:
+                cos, sin = cos * cos_step - sin * sin_step, sin * cos_step + cos * sin_step
+            where = pl.ds(j * LANES, LANES)
+            pick_ref[0, pl.ds(0, subbands), where] = cos.astype(jnp.bfloat16)
+            pick_ref[0, pl.ds(subbands, subbands), where] = (-sin).astype(jnp.bfloat16)
+            pick_ref[1, pl.ds(0, subbands), where] = sin.astype(jnp.bfloat16)
+            pick_ref[1, pl.ds(subbands, subbands), where] = cos.astype(jnp.bfloat16)
+        column = lax.broadcasted_iota(jnp.int32, (ROWS, LANES), 1)
+        column = column // (FRAMES * ROWS) * ROWS + column % ROWS
+        late = jnp.zeros((ROWS, LANES), jnp.int32)
+        for e in range(elems):
+            late = jnp.where(column == e, delay_ref[e], late)
+        late = jnp.concatenate([late] * (subbands // ROWS), axis=0)
+        cos_late, sin_late = cosine(wanted * late, chan), sine(wanted * late, chan)
+
+        span = FRAMES * ROWS
+
+        def pick(first, size):
+            both = sum(
+                lax.dot_general(
+                    pick_ref[r],
+                    wave_ref[r, pl.ds(first, size)],
+                    NT,
+                    preferred_element_type=jnp.float32,
+                )
+                for r in range(parts)
+            )
+            both = [both]
+            if first:
+                both = [jnp.zeros((2 * subbands, first), jnp.float32), *both]
+            if first + size < LANES:
+                both.append(jnp.zeros((2 * subbands, LANES - first - size), jnp.float32))
+            return jnp.concatenate(both, axis=1)
+
+        units = parts * pairs
+        todo = [[] for _ in range(groups * units)]
+        for p in range(1, pairs):
+            todo[p - 1].append((0, p))
+        for n in range(1, groups):
+            for p in range(pairs):
+                todo[n * units + p - 1].append((n, p))
+        both = None
+        for n, g in enumerate(order):
+            volt_copies[n + parts - 1 if n else 0].wait()
+            if n == 1:
+                basis_copy.start()
+                weight_copy.start()
+            if n + 1 < groups:
+                plans.append(turn_plan(order[n + 1], delay_ref))
+            early = plans[n][1].astype(jnp.int32)
+            early = jnp.concatenate([early, jnp.zeros_like(early)], axis=1) != 0
+            if n == groups - 2:
+                chosen = pick(span, n * span)
+            if n == groups - 1:
+                chosen = chosen + pick(n * span, span)
+            for r in range(parts):
+                if n == 0 and r:
+                    volt_copies[r].wait()
+                for p in range(pairs):
+                    filter_pair(g, r, n, p, n % 2, early, volt_ref, coef_ref, wave_ref)
+                    for unit, q in todo[n * units + r * pairs + p]:
+                        turn_pair(q, unit % 2, plans[unit], wide_ref, spun_ref, coef_ref)
+        final = pick(0, span)
+        chosen = jnp.where(lax.broadcasted_iota(jnp.int32, final.shape, 1) < span, final, chosen)
+        real = chosen[:subbands] * cos_late - chosen[subbands:] * sin_late
+        imag = chosen[subbands:] * cos_late + chosen[:subbands] * sin_late
+        for c in range(nchan):
+            part = slice(c * block, (c + 1) * block)
+            send_ref[c] = jnp.concatenate([real[part], imag[part]], axis=0).astype(jnp.bfloat16)
+
+        pl.semaphore_wait(barrier, count - 1)
+
+        def send(other, c):
+            pltpu.make_async_remote_copy(
+                src_ref=send_ref.at[c],
+                dst_ref=recv_ref.at[me],
+                send_sem=send_sem,
+                recv_sem=recv_sem.at[my_set],
+                device_id=other,
+                device_id_type=LOGICAL,
+            ).start()
+
+        each_partner(send)
+        recv_ref[me] = send_ref[chan_at]
+
+        lanes = chan // RADIX
+        wave = [wave_ref[r] for r in range(2)]
+        split_wave = [
+            tuple(wave[r][:, a * lanes : (a + 1) * lanes].astype(jnp.float32) for r in range(2))
+            for a in range(RADIX)
+        ]
+        classes = eight_points(split_wave)
+        basis_copy.wait()
+        powers = []
+        for c in range(RADIX):
+            mixed = jnp.concatenate(classes[c], axis=1).astype(jnp.bfloat16)
+            spec = jnp.dot(mixed, basis_ref[c], preferred_element_type=jnp.float32)
+            both = spec[:, :lanes] * spec[:, :lanes] + spec[:, lanes:] * spec[:, lanes:]
+            totals = []
+            for g in range(groups):
+                tiles = [
+                    both[(g * FRAMES + f) * ROWS : (g * FRAMES + f + 1) * ROWS] for f in range(FRAMES)
+                ]
+                totals.append(sum(tiles[1:], tiles[0]))
+            powers.append(jnp.concatenate(totals, axis=0) * (1.0 / FRAMES))
+        wide = lanes // RADIX
+        at = lax.broadcasted_iota(jnp.int32, (elems, lanes), 1)
+        mixed = []
+        for e in range(RADIX):
+            piece = None
+            for c in range(RADIX):
+                shift = (wide * (c - e)) % lanes
+                moved = pltpu.roll(powers[c], shift, 1) if shift else powers[c]
+                piece = moved if piece is None else jnp.where(at // wide == c, moved, piece)
+            mixed.append(piece)
+        mixed = jnp.concatenate(mixed, axis=0).astype(jnp.bfloat16)
+        down = lax.broadcasted_iota(jnp.int32, (lanes, lanes), 0)
+        over = lax.broadcasted_iota(jnp.int32, (lanes, lanes), 1)
+        back = (over == (down % wide) * RADIX + down // wide).astype(jnp.float32)
+        final = jnp.dot(mixed, back.astype(jnp.bfloat16), preferred_element_type=jnp.float32)
+        for e in range(RADIX):
+            power_ref[:, e * lanes : (e + 1) * lanes] = final[e * elems : (e + 1) * elems].astype(
+                jnp.bfloat16
+            )
+
+        down = lax.broadcasted_iota(jnp.int32, (weight_rows, block * wide_beams), 0)
+        over = lax.broadcasted_iota(jnp.int32, (weight_rows, block * wide_beams), 1)
+        target = down % block * wide_beams + down // block % 2 * (wide_beams // 2)
+        sort = (over == target + down // (2 * block)).astype(jnp.float32).astype(jnp.bfloat16)
+        weight_copy.wait()
+        step = min(8, beams)
+        for i in range(0, beams, step):
+            piece = raw_ref[i : i + step].reshape(step * 2 * block, raw_ref.shape[3])
+            weight_ref[2 * block * i : 2 * block * (i + step)] = piece
+
+        def turn_weights(q, carry):
+            depth = min(total, 8 * LANES)
+            where = pl.multiple_of(q * depth, depth)
+            turned = lax.dot_general(
+                weight_ref[:, pl.ds(where, depth)], sort, TN, preferred_element_type=jnp.float32
+            )
+            for z in range(0, depth, LANES):
+                tiles = [
+                    turned[z + (i * groups + g) * ROWS : z + (i * groups + g + 1) * ROWS]
+                    for g in range(groups)
+                    for i in range(fan)
+                ]
+                turned_ref[pl.ds(pl.multiple_of(where + z, LANES), LANES), :] = jnp.concatenate(
+                    tiles, axis=0
+                ).astype(jnp.bfloat16)
+            return carry
+
+        if total <= 8 * LANES:
+            turn_weights(0, 0)
+        else:
+            lax.fori_loop(0, total // (8 * LANES), turn_weights, 0)
+
+    pl.run_scoped(
+        front, pltpu.SemaphoreType.DMA((5,)), pltpu.SemaphoreType.DMA((groups + parts - 1,))
+    )
 
     sets = count // gather
     place_at = lax.broadcasted_iota(jnp.int32, (2 * block, LANES), 1) // ROWS % fan
@@ -485,7 +488,6 @@
     beams, _, block, total = beam_weights.shape
     basis = class_basis(chan)
     count = nelem * nchan
-    chunks = parts * elems // ROWS
     gather = 8
     wide_beams = max(LANES, 2 * beams)
     out_shape = [
@@ -500,7 +502,7 @@
         scratch_shapes=[
             pltpu.SMEM(delays.shape, jnp.int32),
             pltpu.SMEM(subband_map.shape, jnp.int32),
-            pltpu.VMEM((chunks, ROWS, samples), jnp.bfloat16),
+            pltpu.VMEM((elems // ROWS, parts, ROWS, samples), jnp.bfloat16),
             pltpu.VMEM((taps, chan), jnp.bfloat16),
             pltpu.VMEM(beam_weights.shape, jnp.bfloat16),
             pltpu.VMEM(basis.shape, jnp.bfloat16),
@@ -513,8 +515,6 @@
             pltpu.VMEM((total, block * wide_beams), jnp.bfloat16),
             pltpu.VMEM((nchan, 2 * block, FRAMES * elems), jnp.bfloat16),
             pltpu.VMEM((count, 2 * block, FRAMES * elems), jnp.bfloat16),
-            pltpu.SemaphoreType.DMA((5,)),
-            pltpu.SemaphoreType.DMA((chunks,)),
             pltpu.SemaphoreType.DMA,
             pltpu.SemaphoreType.DMA((count // gather,)),
         ],

time: 13.4 us -> 12.7 us (0.948)
  Pallas kernels: 12.7 us -> 11.9 us
    pallas_call x1, Pallas kernels: 12 us -> 11.3 us  [on_device(): pl.pallas_call(functools.partial(main_kernel, nelem, nchan, gather), in_s...]
where the time goes in v3:
time: 12.7 us; the launch traced here: 12.6 us
  Pallas kernels  11.9 us (94%)
  between operations  0.64 us (5%)
    pallas_call x1, Pallas kernels, on_device(): pl.pallas_call(functools.partial(main_kernel, nelem, nchan, gather), in_s...  11.3 us
    pallas_call x1, Pallas kernels, on_device(): pl.pallas_call(deliver_kernel, in_specs=[pl.BlockSpec(memory_space=pl.ANY...  0.65 us

profile of v3, /device:TPU:0, one launch (start us, length us, event | category | flops | bytes accessed | tf_op | source)
XLA Modules:
  0.0 12.6 jit_solution(4166827032166966540)
XLA Ops:
  0.6 11.3 %shard_map.77 = (bf16[32,1024]{1,0:T(8,128)(2,1)S(1)}, f32[2,16,64]{2,1,0:T(8,128)S(1)}) custom-call(s32[32]{0:T(128)} %delay_hbm.1, s32[16]{0:T(128)} %map_hbm.1, bf16[2,32,19584]{2,1,0:T(8,128)(2,1)} %volt_hbm.1, bf16[16,1024]{1,0:T(8,128)(2,1)} %proto_hbm.1, bf16[64,2,4,1024]{3,2,1,0:T(4,128)(2,1)} %weight_hbm.1, bf16[8,256,256]{2,1,0:T(8,128)(2,1)} %constant.2.clone.basis_hbm), custom_call_target="tpu_custom_call" | custom-call | tf_op jit(solution)/shard_map/pallas_call | solution.py:497
  11.9 0.7 %shard_map.78 = (bf16[32,1024]{1,0:T(8,128)(2,1)}, f32[2,16,64]{2,1,0:T(8,128)}) custom-call(bf16[32,1024]{1,0:T(8,128)(2,1)S(1)} %get-tuple-element.4.power_from, f32[2,16,64]{2,1,0:T(8,128)S(1)} %get-tuple-element.5.beam_from), custom_call_target="tpu_custom_call" | custom-call | tf_op jit(solution)/shard_map/pallas_call | solution.py:525

commit v4 on v3

--- a/solution.py
+++ b/solution.py
@@ -66,27 +66,28 @@
     shift = jnp.zeros((ROWS, LANES), jnp.int32)
     for i in range(ROWS):
         shift = jnp.where(sub == i, delay_ref[group * ROWS + i], shift)
-    return (lane - shift) & (LANES - 1), lane < shift
-
-
-def turn_pair(pair, slot, plan, proto_ref, turned_ref, coef_ref):
-    index, early = plan
+    return (lane - shift) & (LANES - 1), lane < LANES - shift, lane < shift
+
+
+def turn_pair(pair, slot, plan, proto_ref, coef_ref):
+    index, stay, _ = plan
     taps, chan = proto_ref.shape
     per = chan // LANES
-    first, last = 2 * pair, min(2 * pair + 2, per - 1)
-    fresh = [*range(first, last), per - 1] if pair == 0 else range(first, last)
     for t in range(taps):
-        for j in fresh:
-            where = pl.ds(j * LANES, LANES)
-            value = jnp.broadcast_to(proto_ref[pl.ds(t, 1), where], (ROWS, LANES))
-            turned_ref[t, :, where] = jnp.take_along_axis(
-                value, index, axis=1, mode="promise_in_bounds"
-            )
         near = [
-            turned_ref[t, :, pl.ds((first + i) % per * LANES, LANES)] for i in (-1, 0, 1)
+            jnp.broadcast_to(
+                proto_ref[pl.ds(t, 1), pl.ds((2 * pair + i) % per * LANES, LANES)], (ROWS, LANES)
+            )
+            for i in (-1, 0, 1)
         ]
-        coef_ref[slot, t, :, pl.ds(first * LANES, 2 * LANES)] = jnp.concatenate(
-            [jnp.where(early, near[0], near[1]), jnp.where(early, near[1], near[2])], axis=1
+        turned = [
+            jnp.take_along_axis(
+                jnp.where(stay, near[i + 1], near[i]), index, axis=1, mode="promise_in_bounds"
+            )
+            for i in range(2)
+        ]
+        coef_ref[slot, t, :, pl.ds(2 * pair * LANES, 2 * LANES)] = jnp.concatenate(
+            turned, axis=1
         ).astype(jnp.bfloat16)
 
 
@@ -139,7 +140,6 @@
     raw_ref,
     basis_ref,
     wide_ref,
-    spun_ref,
     coef_ref,
     pick_ref,
     wave_ref,
@@ -210,14 +210,14 @@
         proto_copy.start()
         delay_copy.start()
         map_copy.start()
-        for copy in volt_copies[:parts]:
+        for copy in volt_copies[: parts + 1]:
             copy.start()
 
         def greet(other, c):
             pl.semaphore_signal(barrier, inc=1, device_id=other, device_id_type=LOGICAL)
 
         each_partner(greet)
-        for copy in volt_copies[parts:]:
+        for copy in volt_copies[parts + 1 :]:
             copy.start()
 
         map_copy.wait()
@@ -225,8 +225,8 @@
         proto_copy.wait()
         wide_ref[...] = proto_ref[...].astype(jnp.float32)
         pairs = per // 2
-        plans = [turn_plan(order[0], delay_ref)]
-        turn_pair(0, 0, plans[0], wide_ref, spun_ref, coef_ref)
+        plans = [turn_plan(g, delay_ref) for g in order]
+        turn_pair(0, 0, plans[0], wide_ref, coef_ref)
         row = lax.broadcasted_iota(jnp.int32, (subbands, LANES), 0)
         lane = lax.broadcasted_iota(jnp.int32, (subbands, LANES), 1)
         wanted = jnp.zeros((subbands, LANES), jnp.int32)
@@ -276,28 +276,29 @@
             todo[p - 1].append((0, p))
         for n in range(1, groups):
             for p in range(pairs):
-                todo[n * units + p - 1].append((n, p))
+                todo[min(n, 2) * units - pairs + p].append((n, p))
         both = None
         for n, g in enumerate(order):
-            volt_copies[n + parts - 1 if n else 0].wait()
-            if n == 1:
+            if n < groups - 1:
+                volt_copies[n + parts - 1 if n else 0].wait()
+            if n == groups - 2:
                 basis_copy.start()
                 weight_copy.start()
-            if n + 1 < groups:
-                plans.append(turn_plan(order[n + 1], delay_ref))
-            early = plans[n][1].astype(jnp.int32)
+            early = plans[n][2].astype(jnp.int32)
             early = jnp.concatenate([early, jnp.zeros_like(early)], axis=1) != 0
-            if n == groups - 2:
-                chosen = pick(span, n * span)
-            if n == groups - 1:
-                chosen = chosen + pick(n * span, span)
             for r in range(parts):
                 if n == 0 and r:
                     volt_copies[r].wait()
+                if n == groups - 2 and r == parts - 1:
+                    volt_copies[-1].wait()
+                if n == groups - 2 and r == parts - 1:
+                    chosen = pick(span, n * span)
+                if n == groups - 1 and r == 0:
+                    chosen = chosen + pick(n * span, span)
                 for p in range(pairs):
-                    filter_pair(g, r, n, p, n % 2, early, volt_ref, coef_ref, wave_ref)
+                    filter_pair(g, r, n, p, n, early, volt_ref, coef_ref, wave_ref)
                     for unit, q in todo[n * units + r * pairs + p]:
-                        turn_pair(q, unit % 2, plans[unit], wide_ref, spun_ref, coef_ref)
+                        turn_pair(q, unit, plans[unit], wide_ref, coef_ref)
         final = pick(0, span)
         chosen = jnp.where(lax.broadcasted_iota(jnp.int32, final.shape, 1) < span, final, chosen)
         real = chosen[:subbands] * cos_late - chosen[subbands:] * sin_late
@@ -507,8 +508,7 @@
             pltpu.VMEM(beam_weights.shape, jnp.bfloat16),
             pltpu.VMEM(basis.shape, jnp.bfloat16),
             pltpu.VMEM((taps, chan), jnp.float32),
-            pltpu.VMEM((taps, ROWS, chan), jnp.float32),
-            pltpu.VMEM((2, taps, ROWS, chan), jnp.bfloat16),
+            pltpu.VMEM((elems // ROWS, taps, ROWS, chan), jnp.bfloat16),
             pltpu.VMEM((2, 2 * subband_map.shape[0], chan), jnp.bfloat16),
             pltpu.VMEM((parts, FRAMES * elems, chan), jnp.bfloat16),
             pltpu.VMEM((beams * 2 * block, total), jnp.bfloat16),

time: 12.7 us -> 12.5 us (0.984)
  Pallas kernels: 11.9 us -> 11.7 us
    pallas_call x1, Pallas kernels: 11.3 us -> 11.1 us  [on_device(): pl.pallas_call(functools.partial(main_kernel, nelem, nchan, gather), in_s...]
where the time goes in v4:
time: 12.5 us; the launch traced here: 12.4 us
  Pallas kernels  11.7 us (94%)
  between operations  0.64 us (5%)
    pallas_call x1, Pallas kernels, on_device(): pl.pallas_call(functools.partial(main_kernel, nelem, nchan, gather), in_s...  11.1 us
    pallas_call x1, Pallas kernels, on_device(): pl.pallas_call(deliver_kernel, in_specs=[pl.BlockSpec(memory_space=pl.ANY...  0.65 us

profile of v4, /device:TPU:0, one launch (start us, length us, event | category | flops | bytes accessed | tf_op | source)
XLA Modules:
  0.0 12.4 jit_solution(2983761737824111780)
XLA Ops:
  0.6 11.1 %shard_map.77 = (bf16[32,1024]{1,0:T(8,128)(2,1)S(1)}, f32[2,16,64]{2,1,0:T(8,128)S(1)}) custom-call(s32[32]{0:T(128)} %delay_hbm.1, s32[16]{0:T(128)} %map_hbm.1, bf16[2,32,19584]{2,1,0:T(8,128)(2,1)} %volt_hbm.1, bf16[16,1024]{1,0:T(8,128)(2,1)} %proto_hbm.1, bf16[64,2,4,1024]{3,2,1,0:T(4,128)(2,1)} %weight_hbm.1, bf16[8,256,256]{2,1,0:T(8,128)(2,1)} %constant.2.clone.basis_hbm), custom_call_target="tpu_custom_call" | custom-call | tf_op jit(solution)/shard_map/pallas_call | solution.py:498
  11.7 0.7 %shard_map.78 = (bf16[32,1024]{1,0:T(8,128)(2,1)}, f32[2,16,64]{2,1,0:T(8,128)}) custom-call(bf16[32,1024]{1,0:T(8,128)(2,1)S(1)} %get-tuple-element.4.power_from, f32[2,16,64]{2,1,0:T(8,128)S(1)} %get-tuple-element.5.beam_from), custom_call_target="tpu_custom_call" | custom-call | tf_op jit(solution)/shard_map/pallas_call | solution.py:525

commit v5 on v4

--- a/solution.py
+++ b/solution.py
@@ -224,6 +224,7 @@
         delay_copy.wait()
         proto_copy.wait()
         wide_ref[...] = proto_ref[...].astype(jnp.float32)
+        still = jnp.where(me < 0, 1, 0)
         pairs = per // 2
         plans = [turn_plan(g, delay_ref) for g in order]
         turn_pair(0, 0, plans[0], wide_ref, coef_ref)
@@ -274,10 +275,11 @@
         todo = [[] for _ in range(groups * units)]
         for p in range(1, pairs):
             todo[p - 1].append((0, p))
-        for n in range(1, groups):
-            for p in range(pairs):
-                todo[min(n, 2) * units - pairs + p].append((n, p))
-        both = None
+        later = [(n, p) for n in range(1, groups) for p in range(pairs)]
+        ahead = [[] for _ in range(groups * units)]
+        ahead[pairs - 1], later = later[: pairs - 1], later[pairs - 1 :]
+        ahead[2 * pairs - 1], later = later[:1], later[1:]
+        ahead[units + parts * pairs - 1] = later
         for n, g in enumerate(order):
             if n < groups - 1:
                 volt_copies[n + parts - 1 if n else 0].wait()
@@ -296,6 +298,8 @@
                 if n == groups - 1 and r == 0:
                     chosen = chosen + pick(n * span, span)
                 for p in range(pairs):
+                    for unit, q in ahead[n * units + r * pairs + p]:
+                        turn_pair(q, unit + still, plans[unit], wide_ref, coef_ref)
                     filter_pair(g, r, n, p, n, early, volt_ref, coef_ref, wave_ref)
                     for unit, q in todo[n * units + r * pairs + p]:
                         turn_pair(q, unit, plans[unit], wide_ref, coef_ref)
@@ -472,15 +476,18 @@
     return jnp.asarray(np.stack(out), jnp.bfloat16)
 
 
-def deliver_kernel(power_from, beam_from, power_to, beam_to, sems):
-    copies = [
-        pltpu.make_async_copy(power_from, power_to, sems.at[0]),
-        pltpu.make_async_copy(beam_from, beam_to, sems.at[1]),
-    ]
-    for copy in copies:
-        copy.start()
-    for copy in copies:
-        copy.wait()
+def deliver_kernel(power_from, beam_from, power_to, beam_to):
+    def deliver(sems):
+        copies = [
+            pltpu.make_async_copy(power_from, power_to, sems.at[0]),
+            pltpu.make_async_copy(beam_from, beam_to, sems.at[1]),
+        ]
+        for copy in copies:
+            copy.start()
+        for copy in copies:
+            copy.wait()
+
+    pl.run_scoped(deliver, pltpu.SemaphoreType.DMA((2,)))
 
 
 def on_device(nelem, nchan, voltages, delays, prototype, subband_map, beam_weights):
@@ -527,7 +534,6 @@
         in_specs=[pl.BlockSpec(memory_space=pl.ANY)] * 2,
         out_specs=[pl.BlockSpec(memory_space=pl.ANY)] * 2,
         out_shape=out_shape,
-        scratch_shapes=[pltpu.SemaphoreType.DMA((2,))],
         compiler_params=pltpu.CompilerParams(vmem_limit_bytes=2**20),
     )(power, beam)
 

time: 12.5 us -> 12.5 us (level)
  no operation moved by 1% of the time
where the time goes in v5:
time: 12.5 us; the launch traced here: 12.3 us
  Pallas kernels  11.7 us (94%)
  between operations  0.64 us (5%)
    pallas_call x1, Pallas kernels, on_device(): pl.pallas_call(functools.partial(main_kernel, nelem, nchan, gather), in_s...  11 us
    pallas_call x1, Pallas kernels, on_device(): pl.pallas_call(deliver_kernel, in_specs=[pl.BlockSpec(memory_space=pl.ANY...  0.63 us

profile of v5, /device:TPU:0, one launch (start us, length us, event | category | flops | bytes accessed | tf_op | source)
XLA Modules:
  0.0 12.3 jit_solution(3971388354970206449)
XLA Ops:
  0.6 11.0 %shard_map.77 = (bf16[32,1024]{1,0:T(8,128)(2,1)S(1)}, f32[2,16,64]{2,1,0:T(8,128)S(1)}) custom-call(s32[32]{0:T(128)} %delay_hbm.1, s32[16]{0:T(128)} %map_hbm.1, bf16[2,32,19584]{2,1,0:T(8,128)(2,1)} %volt_hbm.1, bf16[16,1024]{1,0:T(8,128)(2,1)} %proto_hbm.1, bf16[64,2,4,1024]{3,2,1,0:T(4,128)(2,1)} %weight_hbm.1, bf16[8,256,256]{2,1,0:T(8,128)(2,1)} %constant.2.clone.basis_hbm), custom_call_target="tpu_custom_call" | custom-call | tf_op jit(solution)/shard_map/pallas_call | solution.py:505
  11.7 0.6 %shard_map.78 = (bf16[32,1024]{1,0:T(8,128)(2,1)}, f32[2,16,64]{2,1,0:T(8,128)}) custom-call(bf16[32,1024]{1,0:T(8,128)(2,1)S(1)} %get-tuple-element.4.power_from, f32[2,16,64]{2,1,0:T(8,128)S(1)} %get-tuple-element.5.beam_from), custom_call_target="tpu_custom_call" | custom-call | tf_op jit(solution)/shard_map/pallas_call | solution.py:532

commit v6 on v5

--- a/solution.py
+++ b/solution.py
@@ -145,6 +145,7 @@
     wave_ref,
     weight_ref,
     turned_ref,
+    swapped_ref,
     send_ref,
     recv_ref,
     send_sem,
@@ -185,6 +186,9 @@
     weight_rows, total = weight_ref.shape
     wide_beams = turned_ref.shape[1] // block
     fan = LANES // elems
+    sets = count // gather
+    depth = gather * elems
+    few = sets <= 8
 
     def front(local_sem, volt_sem):
         order = [*range(1, groups), 0]
@@ -397,16 +401,22 @@
             turn_weights(0, 0)
         else:
             lax.fori_loop(0, total // (8 * LANES), turn_weights, 0)
+        if few:
+            final_set = pl.multiple_of(jnp.where(near_start, sets - 1, 0) * depth, depth)
+            for b in range(block):
+                where = pl.ds(b * wide_beams, wide_beams)
+                tile = turned_ref[pl.ds(final_set, depth), where].astype(jnp.float32)
+                swapped_ref[:, where] = pltpu.roll(tile, wide_beams // 2, 1).astype(jnp.bfloat16)
 
     pl.run_scoped(
         front, pltpu.SemaphoreType.DMA((5,)), pltpu.SemaphoreType.DMA((groups + parts - 1,))
     )
 
-    sets = count // gather
     place_at = lax.broadcasted_iota(jnp.int32, (2 * block, LANES), 1) // ROWS % fan
     low_row = lax.broadcasted_iota(jnp.int32, (2 * block, wide_beams), 0)
 
-    def take(k, carry):
+    def take(k, carry, swap=None):
+        before = swap_of(carry) if swap is not None else None
         which = jnp.where(near_start, k, sets - 1 - k)
         first = which * gather
 
@@ -429,31 +439,38 @@
         picked = jnp.concatenate(
             [jnp.concatenate(p, axis=1) for p in pieces], axis=0
         ).astype(jnp.bfloat16)
-        depth = gather * elems
         where = pl.multiple_of(which * depth, depth)
-        product = jnp.dot(
-            picked, turned_ref[pl.ds(where, depth), :], preferred_element_type=jnp.float32
-        )
-        out = []
-        for f in range(FRAMES):
-            tile = product[2 * block * f : 2 * block * (f + 1)]
-            piece = tile[:, :wide_beams]
-            for s in range(1, block):
-                piece = jnp.where(
-                    low_row % block == s, tile[:, s * wide_beams : (s + 1) * wide_beams], piece
-                )
-            out.append(piece if carry is None else carry[f] + piece)
-        return tuple(out)
-
-    if sets <= 8:
-        sums = None
+
+        def through(weights):
+            product = jnp.dot(picked, weights, preferred_element_type=jnp.float32)
+            out = []
+            for f in range(FRAMES):
+                tile = product[2 * block * f : 2 * block * (f + 1)]
+                piece = tile[:, :wide_beams]
+                for s in range(1, block):
+                    own = tile[:, s * wide_beams : (s + 1) * wide_beams]
+                    piece = jnp.where(low_row % block == s, own, piece)
+                out.append(piece)
+            return out
+
+        out = through(turned_ref[pl.ds(where, depth), :])
+        if swap is not None:
+            swap += [s + o for s, o in zip(before, through(swapped_ref[...]))]
+        return tuple(o if carry is None else c + o for c, o in zip(carry or out, out))
+
+    def swap_of(values):
+        return [pltpu.roll(v, wide_beams // 2, 1) for v in values]
+
+    if few:
+        sums, others = None, []
         for k in range(sets):
-            sums = take(k, sums)
+            sums = take(k, sums, others if k == sets - 1 else None)
     else:
         zero = jnp.zeros((2 * block, wide_beams), jnp.float32)
         sums = lax.fori_loop(0, sets, take, (zero,) * FRAMES)
+        others = swap_of(sums)
     for f in range(FRAMES):
-        other = pltpu.roll(pltpu.roll(sums[f], wide_beams // 2, 1), block, 0)
+        other = pltpu.roll(others[f], block, 0)
         out = sums[f] + jnp.where(low_row < block, -other, other)
         for p in range(2):
             for s in range(block):
@@ -520,6 +537,7 @@
             pltpu.VMEM((parts, FRAMES * elems, chan), jnp.bfloat16),
             pltpu.VMEM((beams * 2 * block, total), jnp.bfloat16),
             pltpu.VMEM((total, block * wide_beams), jnp.bfloat16),
+            pltpu.VMEM((gather * elems, block * wide_beams), jnp.bfloat16),
             pltpu.VMEM((nchan, 2 * block, FRAMES * elems), jnp.bfloat16),
             pltpu.VMEM((count, 2 * block, FRAMES * elems), jnp.bfloat16),
             pltpu.SemaphoreType.DMA,

time: 12.5 us -> 12.4 us (level)
  no operation moved by 1% of the time
where the time goes in v6:
time: 12.4 us; the launch traced here: 12.3 us
  Pallas kernels  11.6 us (94%)
  between operations  0.64 us (5%)
    pallas_call x1, Pallas kernels, on_device(): pl.pallas_call(functools.partial(main_kernel, nelem, nchan, gather), in_s...  11 us
    pallas_call x1, Pallas kernels, on_device(): pl.pallas_call(deliver_kernel, in_specs=[pl.BlockSpec(memory_space=pl.ANY...  0.63 us

profile of v6, /device:TPU:0, one launch (start us, length us, event | category | flops | bytes accessed | tf_op | source)
XLA Modules:
  0.0 12.3 jit_solution(16241094045555750022)
XLA Ops:
  0.6 11.0 %shard_map.77 = (bf16[32,1024]{1,0:T(8,128)(2,1)S(1)}, f32[2,16,64]{2,1,0:T(8,128)S(1)}) custom-call(s32[32]{0:T(128)} %delay_hbm.1, s32[16]{0:T(128)} %map_hbm.1, bf16[2,32,19584]{2,1,0:T(8,128)(2,1)} %volt_hbm.1, bf16[16,1024]{1,0:T(8,128)(2,1)} %proto_hbm.1, bf16[64,2,4,1024]{3,2,1,0:T(4,128)(2,1)} %weight_hbm.1, bf16[8,256,256]{2,1,0:T(8,128)(2,1)} %constant.2.clone.basis_hbm), custom_call_target="tpu_custom_call" | custom-call | tf_op jit(solution)/shard_map/pallas_call | solution.py:522
  11.7 0.6 %shard_map.78 = (bf16[32,1024]{1,0:T(8,128)(2,1)}, f32[2,16,64]{2,1,0:T(8,128)}) custom-call(bf16[32,1024]{1,0:T(8,128)(2,1)S(1)} %get-tuple-element.4.power_from, f32[2,16,64]{2,1,0:T(8,128)S(1)} %get-tuple-element.5.beam_from), custom_call_target="tpu_custom_call" | custom-call | tf_op jit(solution)/shard_map/pallas_call | solution.py:550

commit v7 on v5

--- a/solution.py
+++ b/solution.py
@@ -228,29 +228,31 @@
         pairs = per // 2
         plans = [turn_plan(g, delay_ref) for g in order]
         turn_pair(0, 0, plans[0], wide_ref, coef_ref)
-        row = lax.broadcasted_iota(jnp.int32, (subbands, LANES), 0)
-        lane = lax.broadcasted_iota(jnp.int32, (subbands, LANES), 1)
-        wanted = jnp.zeros((subbands, LANES), jnp.int32)
-        for s in range(subbands):
-            wanted = jnp.where(row == s, map_ref[s], wanted)
-        scale = chan**-0.5
-        cos, sin = cosine(wanted * lane, chan) * scale, sine(wanted * lane, chan) * scale
-        cos_step, sin_step = cosine(wanted * LANES, chan), sine(wanted * LANES, chan)
-        for j in range(per):
-            if j:
-                cos, sin = cos * cos_step - sin * sin_step, sin * cos_step + cos * sin_step
-            where = pl.ds(j * LANES, LANES)
-            pick_ref[0, pl.ds(0, subbands), where] = cos.astype(jnp.bfloat16)
-            pick_ref[0, pl.ds(subbands, subbands), where] = (-sin).astype(jnp.bfloat16)
-            pick_ref[1, pl.ds(0, subbands), where] = sin.astype(jnp.bfloat16)
-            pick_ref[1, pl.ds(subbands, subbands), where] = cos.astype(jnp.bfloat16)
-        column = lax.broadcasted_iota(jnp.int32, (ROWS, LANES), 1)
-        column = column // (FRAMES * ROWS) * ROWS + column % ROWS
-        late = jnp.zeros((ROWS, LANES), jnp.int32)
-        for e in range(elems):
-            late = jnp.where(column == e, delay_ref[e], late)
-        late = jnp.concatenate([late] * (subbands // ROWS), axis=0)
-        cos_late, sin_late = cosine(wanted * late, chan), sine(wanted * late, chan)
+        def tables():
+            row = lax.broadcasted_iota(jnp.int32, (subbands, LANES), 0)
+            lane = lax.broadcasted_iota(jnp.int32, (subbands, LANES), 1)
+            wanted = jnp.zeros((subbands, LANES), jnp.int32)
+            for s in range(subbands):
+                wanted = jnp.where(row == s, map_ref[s], wanted)
+            scale = chan**-0.5
+            cos, sin = cosine(wanted * lane, chan) * scale, sine(wanted * lane, chan) * scale
+            cos_step, sin_step = cosine(wanted * LANES, chan), sine(wanted * LANES, chan)
+            for j in range(per):
+                if j:
+                    cos, sin = cos * cos_step - sin * sin_step, sin * cos_step + cos * sin_step
+                where = pl.ds(j * LANES, LANES)
+                pick_ref[0, pl.ds(0, subbands), where] = cos.astype(jnp.bfloat16)
+                pick_ref[0, pl.ds(subbands, subbands), where] = (-sin).astype(jnp.bfloat16)
+                pick_ref[1, pl.ds(0, subbands), where] = sin.astype(jnp.bfloat16)
+                pick_ref[1, pl.ds(subbands, subbands), where] = cos.astype(jnp.bfloat16)
+            column = lax.broadcasted_iota(jnp.int32, (ROWS, LANES), 1)
+            column = column // (FRAMES * ROWS) * ROWS + column % ROWS
+            late = jnp.zeros((ROWS, LANES), jnp.int32)
+            for e in range(elems):
+                late = jnp.where(column == e, delay_ref[e], late)
+            late = jnp.concatenate([late] * (subbands // ROWS), axis=0)
+            cos_late, sin_late = cosine(wanted * late, chan), sine(wanted * late, chan)
+            return cos_late, sin_late
 
         span = FRAMES * ROWS
 
@@ -286,6 +288,8 @@
             if n == groups - 2:
                 basis_copy.start()
                 weight_copy.start()
+            if n == 1:
+                cos_late, sin_late = tables()
             early = plans[n][2].astype(jnp.int32)
             early = jnp.concatenate([early, jnp.zeros_like(early)], axis=1) != 0
             for r in range(parts):

time: 12.5 us -> 12.5 us (level)
  no operation moved by 1% of the time
where the time goes in v7:
time: 12.5 us; the launch traced here: 12.4 us
  Pallas kernels  11.7 us (94%)
  between operations  0.64 us (5%)
    pallas_call x1, Pallas kernels, on_device(): pl.pallas_call(functools.partial(main_kernel, nelem, nchan, gather), in_s...  11.1 us
    pallas_call x1, Pallas kernels, on_device(): pl.pallas_call(deliver_kernel, in_specs=[pl.BlockSpec(memory_space=pl.ANY...  0.63 us

profile of v7, /device:TPU:0, one launch (start us, length us, event | category | flops | bytes accessed | tf_op | source)
XLA Modules:
  0.0 12.4 jit_solution(12265855392880286784)
XLA Ops:
  0.6 11.1 %shard_map.77 = (bf16[32,1024]{1,0:T(8,128)(2,1)S(1)}, f32[2,16,64]{2,1,0:T(8,128)S(1)}) custom-call(s32[32]{0:T(128)} %delay_hbm.1, s32[16]{0:T(128)} %map_hbm.1, bf16[2,32,19584]{2,1,0:T(8,128)(2,1)} %volt_hbm.1, bf16[16,1024]{1,0:T(8,128)(2,1)} %proto_hbm.1, bf16[64,2,4,1024]{3,2,1,0:T(4,128)(2,1)} %weight_hbm.1, bf16[8,256,256]{2,1,0:T(8,128)(2,1)} %constant.2.clone.basis_hbm), custom_call_target="tpu_custom_call" | custom-call | tf_op jit(solution)/shard_map/pallas_call | solution.py:509
  11.8 0.6 %shard_map.78 = (bf16[32,1024]{1,0:T(8,128)(2,1)}, f32[2,16,64]{2,1,0:T(8,128)}) custom-call(bf16[32,1024]{1,0:T(8,128)(2,1)S(1)} %get-tuple-element.4.power_from, f32[2,16,64]{2,1,0:T(8,128)S(1)} %get-tuple-element.5.beam_from), custom_call_target="tpu_custom_call" | custom-call | tf_op jit(solution)/shard_map/pallas_call | solution.py:536
